TPU v7x, 32 devices: a whole 2x2x4 slice. The times are simulated.
32 devices in a mesh: wide: 16 (over z, x, core), narrow: 2 (over y).
Axes of the slice: x: 2, y: 2, z: 4, core: 2. Of those that a mesh axis runs over, the one named last changes fastest.
Arguments:
- coords: float32 [3, 16, 2048], P(None, 'narrow', 'wide'), may hold values from -1 to 1
- member: int32 [16, 2048], P('narrow', 'wide'), may hold values 0 or 1
- start_vector: float32 [3, 16, 2048], P(None, 'narrow', 'wide'), may hold values from -6 to 6
- self_block: float32 [3, 3, 16, 2048], P(None, None, 'narrow', 'wide'), may hold values from -3 to 141
- neighbour_block: float32 [6, 3, 3, 16, 2048], P(None, None, None, 'narrow', 'wide'), may hold values from -3 to 3
- neighbours: int32 [6, 16, 2048], P(None, 'narrow', 'wide'), may hold values from 0 to 7, as said below
- coarse_map: int32 [512], replicated, may hold values from 0 to 511, each once
Outputs:
- smoothed: float32 [7, 6, 3, 16, 2048], P(None, None, None, 'narrow', 'wide')
- probe_vector: float32 [3, 16, 2048], P(None, 'narrow', 'wide')
- coarse_basis: float32 [36, 512], P(None, ('wide', 'narrow'))
Inputs may be any that keep to these rules, and one draw needn't show every extreme that they name: `neighbours`: the 6 codes of each node are different. `coarse_map`: each aggregate number appears once.
All inputs are finite; a program needn't handle non-finite values. No bound on the sum of `member` on one device may be relied on, other than what follows from the above.
Results may differ from a plain program's by a relative error of at most 0.0003.
Values sent between devices are 32-bit elements; how exact they have to be, the bound alone decides.
A program may use at most 64 MiB of HBM per device.

v0:
```python
import functools

import jax
import jax.numpy as jnp
from jax import lax
from jax.experimental import pallas as pl
from jax.experimental.pallas import tpu as pltpu
from jax.sharding import PartitionSpec as P

TILE = 8
ITERS = 4
MESH = pl.DeviceIdType.MESH
F32 = jnp.float32
SUMS = 10
FIELDS = 9
START, SELF, NB = 0, 3, 12
STEPS = [(-1, -1), (-1, 0), (-1, 1), (0, -1), (0, 1), (1, -1), (1, 0), (1, 1)]


def roll(x, shift, axis):
    size = x.shape[axis]
    shift = shift % size
    return x if shift == 0 else pltpu.roll(x, shift, axis)


def displaced(v, lcol, rcol, rows, lane, row):
    height, width = v.shape
    first, last = lane == 0, lane == width - 1
    top, bottom = row == 0, row == height - 1
    vl = jnp.where(first, lcol, roll(v, 1, 1))
    vr = jnp.where(last, rcol, roll(v, -1, 1))
    w = jnp.where(bottom, rows[1], rows[6])
    wl = jnp.where(bottom, rows[0], rows[5])
    wr = jnp.where(bottom, rows[2], rows[7])
    wsl = roll(jnp.where(last, wl, w), 1, 1)
    wsr = roll(jnp.where(first, wr, w), -1, 1)
    up = [roll(jnp.where(bottom, b, a), 1, 0) for a, b in ((vl, wsl), (v, w), (vr, wsr))]
    down = [roll(jnp.where(top, b, a), -1, 0) for a, b in ((vl, wsl), (v, w), (vr, wsr))]
    return up + [vl, vr] + down


def kernel(
    wide, narrow, share,
    coords_h, member_h, start_h, self_h, nb_h, nbr_h, cmap_h,
    out_ref, probe_ref, coarse_ref,
    coords, member, nbr, cmap,
    ext, wpack, stencil, fields, pack, tedges, disp, mine, gath, sumrow, allsum, partial,
    wrecv, htrecv, vtrecv,
    in_sem, send_sem, recv_sem, tsend_sem, trecv_sem, gsend_sem, grecv_sem, ssend_sem, srecv_sem,
):
    count = wide * narrow
    me_w, me_n = lax.axis_index("wide"), lax.axis_index("narrow")
    me = me_w * narrow + me_n
    barrier = pltpu.get_barrier_semaphore()

    def peer(d):
        other = lax.rem(me + d, count)
        return (other // narrow, lax.rem(other, narrow))

    @pl.loop(1, count)
    def _(d):
        pl.semaphore_signal(barrier, inc=1, device_id=peer(d), device_id_type=MESH)

    height, width = shape = member.shape
    edge_count = nbr.shape[0]
    codes_at = NB + 9 * edge_count
    planes = codes_at + edge_count

    def own(first, size):
        return ext.at[first : first + size, 0:height, 0:width]

    loads = [
        pltpu.make_async_copy(src, dst, in_sem.at[i])
        for i, (src, dst) in enumerate(
            (
                (nbr_h, nbr), (start_h, own(START, 3)), (self_h, own(SELF, 9)), (nb_h, own(NB, nb_h.shape[0])),
                (coords_h, coords), (member_h, member), (cmap_h, cmap),
            )
        )
    ]
    for load in loads:
        load.start()

    def exists(code):
        dy, dx = STEPS[code]
        ok = None
        for step, at, size in ((dy, me_n, narrow), (dx, me_w, wide)):
            term = at > 0 if step < 0 else (at < size - 1 if step > 0 else None)
            if term is not None:
                ok = term if ok is None else jnp.logical_and(ok, term)
        return ok

    present_at = [exists(code) for code in range(8)]

    def target(code):
        dy, dx = STEPS[code]
        return (me_w + dx, me_n + dy)

    for code in range(8):
        @pl.when(jnp.logical_not(present_at[code]))
        def _(code=code):
            if code in (1, 6):
                at = height + ITERS if code == 1 else height
                ext[:, at : at + ITERS, 0:width] = jnp.zeros((planes, ITERS, width), F32)
            else:
                wrecv[code] = jnp.zeros(wrecv.shape[1:], F32)
            if code in (3, 4):
                htrecv[code - 3] = jnp.zeros(htrecv.shape[1:], F32)
            else:
                vtrecv[code] = jnp.zeros(vtrecv.shape[1:], F32)

    lane = lax.broadcasted_iota(jnp.int32, shape, 1)
    row = lax.broadcasted_iota(jnp.int32, shape, 0)

    for load in loads[:4]:
        load.wait()
    for k in range(edge_count):
        ext[codes_at + k, 0:height, 0:width] = nbr[k].astype(F32)
    per = width // ITERS
    for side in range(2):
        for t in range(wpack.shape[1]):
            tile = jnp.zeros(shape, F32)
            for j, p in enumerate(range(t * per, min((t + 1) * per, planes))):
                moved = roll(ext[p, 0:height, 0:width], ITERS * (j + side), 1)
                tile = jnp.where(lane // ITERS == j, moved, tile)
            wpack[side, t] = tile

    pl.semaphore_wait(barrier, count - 1)

    copies = []
    for code in range(8):
        dx = STEPS[code][1]
        if dx == 0:
            here, there = (0, height) if code == 1 else (height - ITERS, height + ITERS)
            src = ext.at[:, here : here + ITERS, 0:width]
            dst = ext.at[:, there : there + ITERS, 0:width]
        else:
            src, dst = wpack.at[0 if dx < 0 else 1], wrecv.at[7 - code]
        copy = pltpu.make_async_remote_copy(
            src_ref=src, dst_ref=dst, send_sem=send_sem.at[code], recv_sem=recv_sem.at[7 - code],
            device_id=target(code), device_id_type=MESH,
        )
        pl.when(present_at[code])(copy.start)
        copies.append(copy)

    for load in loads[4:]:
        load.wait()
    present = member[...].astype(F32)
    x, y, z = (coords[r] * present for r in range(3))
    products = [present * present, x * present, y * present, z * present, x * x, y * y, z * z, x * y, x * z, y * z]
    tiles = []
    for base in (0, 8):
        tile = jnp.zeros(shape, F32)
        for q, product in enumerate(products[base : base + 8]):
            tile = jnp.where(row == q, jnp.sum(product, axis=0, keepdims=True), tile)
        for s in (1, 2, 4):
            tile = tile + jnp.where((lane & s) != 0, roll(tile, s, 1), roll(tile, -s, 1))
        tiles.append(tile)
    sums = [tiles[q // 8][q % 8 : q % 8 + 1, :] for q in range(SUMS)]

    def factor(sums):
        n, sx, sy, sz, xx, yy, zz, xy, xz, yz = sums
        l00 = jnp.sqrt(n)
        mx, my, mz = sx / l00, sy / l00, sz / l00
        l33 = jnp.sqrt(xx + yy - mx * mx - my * my)
        l43 = (mx * mz - xz) / l33
        l53 = (my * mz - yz) / l33
        l44 = jnp.sqrt(yy + zz - my * my - mz * mz - l43 * l43)
        l54 = (mx * my - xy - l53 * l43) / l44
        l55 = jnp.sqrt(xx + zz - mx * mx - mz * mz - l53 * l53 - l54 * l54)
        return l00, mx, my, mz, l33, l43, l53, l44, l54, l55

    parts = factor(sums)
    l00, mx, my, mz, l33, l43, l53, l44, l54, l55 = parts
    unit = present / l00
    cx, cy, cz = x - mx * unit, y - my * unit, z - mz * unit
    a0, a1 = -cy / l33, cx / l33
    b0, b1, b2 = -l43 * a0 / l44, (-cz - l43 * a1) / l44, cy / l44
    g0 = (cz - l53 * a0 - l54 * b0) / l55
    g1 = (-l53 * a1 - l54 * b1) / l55
    g2 = (-cx - l54 * b2) / l55
    tent = [unit, a0, a1, b0, b1, b2, g0, g1, g2]
    packl, packr = jnp.zeros(shape, F32), jnp.zeros(shape, F32)
    for j, field in enumerate(tent):
        fields[j] = field
        packl = jnp.where(lane == j, roll(field, j, 1), packl)
        packr = jnp.where(lane == j, roll(field, j + 1, 1), packr)
        tedges[0, j : j + 1, :] = field[:1]
        tedges[1, j : j + 1, :] = field[height - 1 :]
    pack[0] = packl
    pack[1] = packr
    lane_row = lax.broadcasted_iota(jnp.int32, (1, width), 1) % 8
    rows_out = []
    for base in (0, 8):
        line = jnp.zeros((1, width), F32)
        for q, part in enumerate(parts[base : base + 8]):
            line = jnp.where(lane_row == q, part, line)
        rows_out.append(line)
    mine[0:1] = rows_out[0]
    mine[1:2] = rows_out[1]
    gath[me] = jnp.concatenate(rows_out, axis=0)

    def wait_halo(codes, recv, ref_of):
        for code in codes:
            ref = ref_of(code)
            arrival = pltpu.make_async_copy(ref, ref, recv.at[code])
            pl.when(present_at[code])(arrival.wait)

    tcopies = []
    for code in range(8):
        if code in (3, 4):
            src, dst = pack.at[code - 3], htrecv.at[4 - code]
        else:
            src, dst = tedges.at[0 if code < 3 else 1], vtrecv.at[7 - code]
        copy = pltpu.make_async_remote_copy(
            src_ref=src, dst_ref=dst, send_sem=tsend_sem.at[code], recv_sem=trecv_sem.at[7 - code],
            device_id=target(code), device_id_type=MESH,
        )
        pl.when(present_at[code])(copy.start)
        tcopies.append(copy)

    @pl.loop(1, count)
    def _(d):
        pltpu.make_async_remote_copy(
            src_ref=mine, dst_ref=gath.at[me], send_sem=gsend_sem, recv_sem=grecv_sem,
            device_id=peer(d), device_id_type=MESH,
        ).start()

    def by_displacement(r0, c0):
        def at(p):
            return ext[p, r0 : r0 + height, c0 : c0 + width]

        for code in range(8):
            masks = [at(codes_at + k) == code for k in range(edge_count)]
            for q in range(9):
                value = jnp.zeros(shape, F32)
                for k in range(edge_count):
                    value = jnp.where(masks[k], at(NB + 9 * k + q), value)
                stencil[code, q, r0 : r0 + height, c0 : c0 + width] = value

    def ring(code):
        at = height + ITERS if code == 1 else height
        return ext.at[:, at : at + ITERS, 0:width]

    by_displacement(0, 0)
    wait_halo((1, 6), recv_sem, ring)
    by_displacement(height, 0)
    wait_halo((0, 2, 3, 4, 5, 7), recv_sem, lambda code: wrecv.at[code])
    half = row < ITERS
    for t in range(wpack.shape[1]):
        pairs = (
            (wrecv[4, t], wrecv[3, t]),
            (jnp.where(half, wrecv[7, t], wrecv[2, t]), jnp.where(half, wrecv[5, t], wrecv[0, t])),
        )
        for j, p in enumerate(range(t * per, min((t + 1) * per, planes))):
            for r0, (right, left) in zip((0, height), pairs):
                tile = jnp.where(lane >= width - ITERS, roll(left, -ITERS * (j + 1), 1), 0.0)
                ext[p, r0 : r0 + height, width:] = jnp.where(lane < ITERS, roll(right, -ITERS * j, 1), tile)
    by_displacement(0, width)
    by_displacement(height, width)

    def full(p):
        return ext[p]

    selfb = {(r, s): (lambda r=r, s=s: ext[SELF + 3 * r + s, 0:height, 0:width]) for r in range(3) for s in range(3)}
    nb = {
        (k, r, s): (lambda k=k, r=r, s=s: ext[NB + 9 * k + 3 * r + s, 0:height, 0:width])
        for k in range(edge_count) for r in range(3) for s in range(3)
    }
    elane = lax.broadcasted_iota(jnp.int32, (2 * height, 2 * width), 1)
    erow = lax.broadcasted_iota(jnp.int32, (2 * height, 2 * width), 0)

    def between(value, low, high):
        return jnp.logical_and(value >= low, value < high)

    last_row = jnp.where(me_n < narrow - 1, height + ITERS, height)
    back_row = jnp.where(me_n > 0, height + ITERS, 2 * height)
    last_lane = jnp.where(me_w < wide - 1, width + ITERS, width)
    back_lane = jnp.where(me_w > 0, 2 * width - ITERS, 2 * width)
    inside = jnp.logical_and(
        jnp.logical_or(erow < last_row, erow >= back_row), jnp.logical_or(elane < last_lane, elane >= back_lane)
    )
    inverse = [jnp.where(inside, 1.0 / full(SELF + 4 * r), 0.0) for r in range(3)]
    diag = [selfb[r, r]() for r in range(3)]
    inv = [inverse[r][:height, :width] for r in range(3)]

    iterate = [full(START + r) for r in range(3)]
    for number in range(ITERS):
        final = number == ITERS - 1
        rs, cs = (slice(0, height), slice(0, width)) if final else (slice(None), slice(None))
        applied = [sum(ext[SELF + 3 * r + s, rs, cs] * iterate[s][rs, cs] for s in range(3)) for r in range(3)]
        for s in range(3):
            for dy in (-1, 0, 1):
                shifted = roll(iterate[s], -dy, 0)
                for dx in (-1, 0, 1):
                    if (dy, dx) == (0, 0):
                        continue
                    code = STEPS.index((dy, dx))
                    moved = roll(shifted, -dx, 1)[rs, cs]
                    for r in range(3):
                        applied[r] = applied[r] + stencil[code, 3 * r + s, rs, cs] * moved
        mine_it = [v[:height, :width] for v in iterate]
        mine_ap = [v[:height, :width] for v in applied]
        curvature = sum(mine_it[r] * mine_ap[r] for r in range(3))
        energy = sum(mine_it[r] * diag[r] * mine_it[r] for r in range(3))
        partial[number : number + 1] = jnp.sum(curvature, axis=0, keepdims=True)
        partial[number + 4 : number + 5] = jnp.sum(energy, axis=0, keepdims=True)
        iterate = [applied[r] * (inv[r] if final else inverse[r]) for r in range(3)]

    totals = jnp.sum(partial[...], axis=1, keepdims=True)
    line = jnp.sum(jnp.where(lane == row, totals, 0.0), axis=0, keepdims=True)
    sumrow[...] = line
    allsum[me] = line

    @pl.loop(1, count)
    def _(d):
        pltpu.make_async_remote_copy(
            src_ref=sumrow, dst_ref=allsum.at[me], send_sem=ssend_sem, recv_sem=srecv_sem,
            device_id=peer(d), device_id_type=MESH,
        ).start()

    wait_halo(range(8), trecv_sem, lambda code: htrecv.at[code - 3] if code in (3, 4) else vtrecv.at[code])
    lpack, rpack = htrecv[0], htrecv[1]
    for j in range(FIELDS):
        rows = {code: vtrecv[code, j : j + 1, :] for code in (0, 1, 2, 5, 6, 7)}
        moved = displaced(tent[j], roll(lpack, -j, 1), roll(rpack, width - 1 - j, 1), rows, lane, row)
        for code in range(8):
            disp[j, code] = moved[code]

    def piece(block, picked, index):
        unit, a0, a1, b0, b1, b2, g0, g1, g2 = picked
        for r in range(3):
            c0, c1, c2 = (block(r, s) * -inv[r] for s in range(3))
            out_ref[index, 0, r] = c0 * unit
            out_ref[index, 1, r] = c1 * unit
            out_ref[index, 2, r] = c2 * unit
            out_ref[index, 3, r] = c0 * a0 + c1 * a1
            out_ref[index, 4, r] = c0 * b0 + c1 * b1 + c2 * b2
            out_ref[index, 5, r] = c0 * g0 + c1 * g1 + c2 * g2

    piece(lambda r, s: selfb[r, s](), [fields[j] for j in range(FIELDS)], 0)
    for k in range(edge_count):
        masks = [nbr[k] == code for code in range(1, 8)]
        picked = []
        for j in range(FIELDS):
            value = disp[j, 0]
            for code in range(1, 8):
                value = jnp.where(masks[code - 1], disp[j, code], value)
            picked.append(value)
        piece(lambda r, s: nb[k, r, s](), picked, k + 1)

    some = gath.at[pl.ds(0, count - 1)]
    pltpu.make_async_copy(some, some, grecv_sem).wait()
    across = width // TILE * wide
    tiles_x, tiles_y = width // TILE, height // TILE
    crow = lax.broadcasted_iota(jnp.int32, (share, width), 0)
    cgroup = lax.broadcasted_iota(jnp.int32, (share, width), 1) // TILE
    low, high = jnp.zeros((share, width), F32), jnp.zeros((share, width), F32)
    for j in range(share):
        wanted = cmap[me * share + j]
        tile_row, tile_col = wanted // across, lax.rem(wanted, across)
        slot = tile_col // tiles_x * narrow + tile_row // tiles_y
        lines = gath[slot]
        take = jnp.logical_and(crow == j, cgroup == lax.rem(tile_col, tiles_x))
        low = jnp.where(take, lines[0:1], low)
        high = jnp.where(take, lines[1:2], high)
    l00, mx, my, mz, l33, l43, l53, l44, l54, l55 = range(SUMS)
    entries = {
        (0, 0): (l00, 1), (1, 1): (l00, 1), (2, 2): (l00, 1),
        (3, 0): (my, -1), (3, 1): (mx, 1), (4, 1): (mz, -1), (4, 2): (my, 1), (5, 0): (mz, 1), (5, 2): (mx, -1),
        (3, 3): (l33, 1), (4, 3): (l43, 1), (5, 3): (l53, 1), (4, 4): (l44, 1), (5, 4): (l54, 1), (5, 5): (l55, 1),
    }
    outs = coarse_ref.shape[1]
    kind = lax.broadcasted_iota(jnp.int32, (1, outs), 1)
    chosen, sign = jnp.full((1, outs), -1, jnp.int32), jnp.zeros((1, outs), F32)
    for (n, m), (q, way) in entries.items():
        chosen = jnp.where(kind == 6 * m + n, q, chosen)
        sign = jnp.where(kind == 6 * m + n, float(way), sign)
    entry = lax.broadcasted_iota(jnp.int32, (width, outs), 0) % 8
    coarse = jnp.zeros(coarse_ref.shape, F32)
    for base, lines in ((0, low), (8, high)):
        pick = jnp.where(entry + base == chosen, sign, 0.0)
        coarse = coarse + jnp.dot(lines, pick, precision=lax.Precision.HIGHEST, preferred_element_type=F32)
    coarse_ref[...] = coarse

    some = allsum.at[pl.ds(0, count - 1)]
    pltpu.make_async_copy(some, some, srecv_sem).wait()
    if count <= 64:
        lines = [allsum[d] for d in range(count)]
        while len(lines) > 1:
            lines = [a + b for a, b in zip(lines[::2], lines[1::2])] + ([lines[-1]] if len(lines) % 2 else [])
        total = lines[0]
    else:
        total = lax.fori_loop(0, count, lambda d, t: t + allsum[d], jnp.zeros((1, width), F32))
    lane1 = lax.broadcasted_iota(jnp.int32, (1, width), 1)
    ratio = roll(jnp.broadcast_to(total, shape), -4, 1)[:1] / total
    ratios = [jnp.sum(jnp.where(lane1 == i, ratio, 0.0), axis=1, keepdims=True) for i in range(ITERS)]
    growth = ratios[0]
    for i in range(1, ITERS):
        growth = growth * ratios[i]
    weight = jnp.broadcast_to(ratios[ITERS - 1] * (4.0 / 3.0), shape)
    growth = jnp.broadcast_to(growth, shape)
    for r in range(3):
        probe_ref[r] = iterate[r] * growth
    base = {(0, 0): 0, (1, 1): 0, (2, 2): 0, (3, 0): 1, (3, 1): 2}
    for r in range(3):
        base[(4, r)] = 3 + r
        base[(5, r)] = 6 + r
    for m in range(6):
        for r in range(3):
            value = out_ref[0, m, r] * weight
            out_ref[0, m, r] = value + fields[base[(m, r)]] if (m, r) in base else value
    for k in range(1, edge_count + 1):
        for m in range(6):
            for r in range(3):
                out_ref[k, m, r] = out_ref[k, m, r] * weight

    for some in (copies, tcopies):
        for code in range(8):
            pl.when(present_at[code])(some[code].wait_send)
    for buffer, sem in ((gath, gsend_sem), (allsum, ssend_sem)):
        some = buffer.at[pl.ds(0, count - 1)]
        pltpu.make_async_copy(some, some, sem).wait()


def local(wide, narrow, coords, member, start_vector, self_block, neighbour_block, neighbours, coarse_map):
    height, width = member.shape
    edge_count = neighbours.shape[0]
    count = wide * narrow
    share = coarse_map.shape[0] // count
    tile = (height, width)
    double = (2 * height, 2 * width)
    planes = 12 + 10 * edge_count
    packs = pl.cdiv(planes, width // ITERS)
    vmem = pltpu.VMEM
    dma = pltpu.SemaphoreType.DMA
    smoothed, probe, coarse = pl.pallas_call(
        functools.partial(kernel, wide, narrow, share),
        out_shape=(
            jax.ShapeDtypeStruct((edge_count + 1, 6, 3) + tile, F32),
            jax.ShapeDtypeStruct((3,) + tile, F32),
            jax.ShapeDtypeStruct((share, 36), F32),
        ),
        in_specs=[pl.BlockSpec(memory_space=pl.ANY)] * 7,
        out_specs=(pl.BlockSpec(memory_space=pltpu.VMEM),) * 3,
        scratch_shapes=[
            vmem((3,) + tile, F32),
            vmem(tile, jnp.int32),
            vmem((edge_count,) + tile, jnp.int32),
            pltpu.SMEM(coarse_map.shape, jnp.int32),
            vmem((planes,) + double, F32),
            vmem((2, packs) + tile, F32),
            vmem((8, 9) + double, F32),
            vmem((FIELDS,) + tile, F32),
            vmem((2,) + tile, F32),
            vmem((2, 16, width), F32),
            vmem((FIELDS, 8) + tile, F32),
            vmem((2, width), F32),
            vmem((count, 2, width), F32),
            vmem((1, width), F32),
            vmem((count, 1, width), F32),
            vmem((8, width), F32),
            vmem((8, packs) + tile, F32),
            vmem((2,) + tile, F32),
            vmem((8, 16, width), F32),
            dma((7,)),
            dma((8,)),
            dma((8,)),
            dma((8,)),
            dma((8,)),
            dma(()),
            dma(()),
            dma(()),
            dma(()),
        ],
        compiler_params=pltpu.CompilerParams(collective_id=0, has_side_effects=True),
    )(
        coords, member, start_vector, self_block.reshape((9,) + tile), neighbour_block.reshape((-1,) + tile),
        neighbours, coarse_map,
    )
    return smoothed, probe, coarse.T


def solution(mesh):
    return jax.shard_map(
        functools.partial(local, mesh.shape["wide"], mesh.shape["narrow"]),
        mesh=mesh,
        in_specs=(
            P(None, "narrow", "wide"),
            P("narrow", "wide"),
            P(None, "narrow", "wide"),
            P(None, None, "narrow", "wide"),
            P(None, None, None, "narrow", "wide"),
            P(None, "narrow", "wide"),
            P(),
        ),
        out_specs=(
            P(None, None, None, "narrow", "wide"),
            P(None, "narrow", "wide"),
            P(None, ("wide", "narrow")),
        ),
        check_vma=False,
    )
```

profile of v0, /device:TPU:0, one launch (start us, length us, event | category | flops | bytes accessed | tf_op | source)
XLA Modules:
  0.0 23.1 jit_solution(10857659955847860108)
XLA Ops:
  0.6 19.2 %shard_map.94 = (f32[7,6,3,8,128]{4,3,2,1,0:T(8,128)}, f32[3,8,128]{2,1,0:T(8,128)}, f32[16,36]{1,0:T(8,128)}) custom-call(f32[3,8,128]{2,1,0:T(8,128)} %coords_h.1, s32[8,128]{1,0:T(8,128)} %member_h.1, f32[3,8,128]{2,1,0:T(8,128)} %start_h.1, f32[9,8,128]{2,1,0:T(8,128)} %bitcast.4, f32[54,8,128]{2,1,0:T(8,128)} %bitcast.3, s32[6,8,128]{2,1,0:T(8,128)} %nbr_h.1, ...), custom_call_target="tpu_custom_call" | custom-call | tf_op jit(solution)/shard_map/pallas_call | solution.py:437
  19.9 0.0 copy-start
  19.9 1.9 %copy.13 = f32[7,6,3,8,128]{4,3,2,1,0:T(8,128)} copy(f32[7,6,3,8,128]{4,3,2,1,0:T(8,128)} %get-tuple-element.12) | data formatting | bytes 1032192
  21.7 0.0 copy-done
  21.7 0.0 copy-start.1
  21.8 0.6 %copy.14 = f32[3,8,128]{2,1,0:T(8,128)} copy(f32[3,8,128]{2,1,0:T(8,128)S(1)} %copy-done) | data formatting | bytes 24576
  22.4 0.1 copy-done.1
  22.5 0.6 %copy.15 = f32[36,16]{0,1:T(8,128)} copy(f32[36,16]{0,1:T(8,128)S(1)} %bitcast.5) | data formatting | bytes 4608
Async XLA Ops:
  19.9 1.9 %copy-start = (f32[3,8,128]{2,1,0:T(8,128)S(1)}, f32[3,8,128]{2,1,0:T(8,128)}, u32[]{:S(2)}) copy-start(f32[3,8,128]{2,1,0:T(8,128)} %get-tuple-element.13) | copy-start | bytes 36868
  21.7 0.7 %copy-start.1 = (f32[16,36]{1,0:T(8,128)S(1)}, f32[16,36]{1,0:T(8,128)}, u32[]{:S(2)}) copy-start(f32[16,36]{1,0:T(8,128)} %get-tuple-element.8) | copy-start | bytes 6916
where the time goes:
time: 23.3 us; the launch traced here: 23.1 us
  Pallas kernels  19.2 us (82%)
  local copies, waits for them, and re-layouts  3.17 us (14%)
  between operations  0.65 us (3%)
    pallas_call x1, Pallas kernels, local(): pl.pallas_call(functools.partial(kernel, wide, narrow, share), out_shape=...  19.2 us
    unnamed x7, local copies, waits for them, and re-layouts  3.17 us

commit v1 on v0

v1 whole, which is shorter than its diff:
```python
import functools

import jax
import jax.numpy as jnp
from jax import lax
from jax.experimental import pallas as pl
from jax.experimental.pallas import tpu as pltpu
from jax.sharding import PartitionSpec as P

TILE = 8
ITERS = 4
MESH = pl.DeviceIdType.MESH
F32 = jnp.float32
SUMS = 10
FIELDS = 9
START, SELF, NB = 0, 3, 12
STEPS = [(-1, -1), (-1, 0), (-1, 1), (0, -1), (0, 1), (1, -1), (1, 0), (1, 1)]
VMEM_LIMIT = 16 * 1024 * 1024


def roll(x, shift, axis):
    size = x.shape[axis]
    shift = shift % size
    return x if shift == 0 else pltpu.roll(x, shift, axis)


def plane_width(wide):
    best = max(size for size in range(1, wide + 1) if wide % size == 0 and size * size <= wide)
    return wide if best == 1 else best


def edge_slots(planes, width):
    slots, tile, at = [], 0, 0
    for p in range(planes):
        columns = ITERS if p < SELF else ITERS - 1
        if at + columns > width:
            tile, at = tile + 1, 0
        slots.append((tile, at, columns))
        at += columns
    return slots, tile + 1


def kernel(
    wide, narrow, share,
    coords_h, member_h, start_h, self_h, nb_h, nbr_h, cmap_h,
    out_ref, fields, iter_ref, scale_ref, coarse_ref,
    coords, member, nbr, cmap,
    ext, wpack, stencil, pack, tedges, disp, mine, gath, sumrow, allsum, partial,
    wrecv, htrecv, vtrecv, ctrecv,
    in_sem, send_sem, recv_sem, tsend_sem, trecv_sem, gsend_sem, grecv_sem, ssend_sem, srecv_sem, far_sem,
):
    count = wide * narrow
    me_w, me_n = lax.axis_index("wide"), lax.axis_index("narrow")
    me = me_w * narrow + me_n
    barrier = pltpu.get_barrier_semaphore()
    across_plane = plane_width(wide)
    plane_count = wide // across_plane
    me_p, me_q = me_w // across_plane, lax.rem(me_w, across_plane)

    height, width = shape = member.shape
    edge_count = nbr.shape[0]
    codes_at = NB + 9 * edge_count
    planes = codes_at + edge_count
    slots, tiles = edge_slots(planes, width)
    right, left = 0, 1

    def exists(code):
        dy, dx = STEPS[code]
        ok = None
        for step, at, size in ((dy, me_n, narrow), (dx, me_w, wide)):
            term = at > 0 if step < 0 else (at < size - 1 if step > 0 else None)
            if term is not None:
                ok = term if ok is None else jnp.logical_and(ok, term)
        return ok

    present_at = [exists(code) for code in range(8)]

    def target(code):
        dy, dx = STEPS[code]
        return (me_w + dx, me_n + dy)

    def greet(cond, device):
        @pl.when(cond)
        def _():
            pl.semaphore_signal(barrier, inc=1, device_id=device, device_id_type=MESH)
        return cond.astype(jnp.int32)

    expected = 0
    for code in (1, 6, 0, 2, 5, 7, 3, 4):
        expected = expected + greet(present_at[code], target(code))

    def own(first, size):
        return ext.at[first : first + size, 0:height, 0:width]

    loads = [
        pltpu.make_async_copy(src, dst, in_sem.at[i])
        for i, (src, dst) in enumerate(
            (
                (nbr_h, nbr), (start_h, own(START, 3)), (self_h, own(SELF, 9)), (nb_h, own(NB, nb_h.shape[0])),
                (coords_h, coords), (member_h, member), (cmap_h, cmap),
            )
        )
    ]
    for load in loads:
        load.start()

    def near(w, n):
        return jnp.logical_and(jnp.abs(w - me_w) <= 1, jnp.abs(n - me_n) <= 1)

    for q in range(across_plane):
        for n in range(narrow):
            w = me_p * across_plane + q
            expected = expected + greet(jnp.logical_not(near(w, n)), (w, n))
    for p in range(plane_count):
        w = p * across_plane + me_q
        expected = expected + greet(jnp.logical_and(p != me_p, jnp.logical_not(near(w, me_n))), (w, me_n))

    for code in range(8):
        dy, dx = STEPS[code]
        @pl.when(jnp.logical_not(present_at[code]))
        def _(code=code, dy=dy, dx=dx):
            side = right if dx > 0 else left
            if dx == 0:
                at = height if dy > 0 else height + ITERS
                ext[:, at : at + ITERS, 0:width] = jnp.zeros((planes, ITERS, width), F32)
                vtrecv[0 if dy < 0 else 1] = jnp.zeros(vtrecv.shape[1:], F32)
            elif dy == 0:
                wrecv[side] = jnp.zeros(wrecv.shape[1:], F32)
                htrecv[side] = jnp.zeros(htrecv.shape[1:], F32)
            else:
                at = 0 if dy > 0 else ITERS
                wrecv[2 + side, :, at : at + ITERS, :] = jnp.zeros((tiles, ITERS, width), F32)
                ctrecv[2 * side + (0 if dy < 0 else 1)] = jnp.zeros(ctrecv.shape[1:], F32)

    lane = lax.broadcasted_iota(jnp.int32, shape, 1)
    row = lax.broadcasted_iota(jnp.int32, shape, 0)

    for load in loads[:4]:
        load.wait()
    for k in range(edge_count):
        ext[codes_at + k, 0:height, 0:width] = nbr[k].astype(F32)
    for side in (right, left):
        packed = [jnp.zeros(shape, F32) for _ in range(tiles)]
        for p, (t, at, columns) in enumerate(slots):
            first = 0 if side == left else width - columns
            moved = roll(ext[p, 0:height, 0:width], at - first, 1)
            packed[t] = moved if at == 0 else jnp.where(lane >= at, moved, packed[t])
        for t in range(tiles):
            wpack[side, t] = packed[t]

    pl.semaphore_wait(barrier, expected)

    pieces_of = {}
    for code in range(8):
        dy, dx = STEPS[code]
        if dx == 0:
            pairs = []
            for first, size, deep in ((START, 3, ITERS), (SELF, planes - SELF, ITERS - 1)):
                here = 0 if dy < 0 else height - deep
                there = height if dy < 0 else height + 2 * ITERS - deep
                pairs.append((
                    ext.at[first : first + size, here : here + deep, 0:width],
                    ext.at[first : first + size, there : there + deep, 0:width],
                ))
        else:
            mine_side, their_side = (left, right) if dx < 0 else (right, left)
            if dy == 0:
                pairs = [(wpack.at[mine_side], wrecv.at[their_side])]
            else:
                at = 0 if dy < 0 else ITERS
                pairs = [(
                    wpack.at[mine_side, :, at : at + ITERS, :], wrecv.at[2 + their_side, :, at : at + ITERS, :],
                )]
        pieces_of[code] = pairs

    copies = {}
    for code in (1, 6, 0, 2, 5, 7, 3, 4):
        made = [
            pltpu.make_async_remote_copy(
                src_ref=src, dst_ref=dst, send_sem=send_sem.at[code, i], recv_sem=recv_sem.at[7 - code, i],
                device_id=target(code), device_id_type=MESH,
            )
            for i, (src, dst) in enumerate(pieces_of[code])
        ]

        @pl.when(present_at[code])
        def _(made=made):
            for copy in made:
                copy.start()
        copies[code] = made

    for p in range(plane_count):
        @pl.when(p != me_p)
        def _(p=p):
            pl.semaphore_signal(
                far_sem, inc=1, device_id=(p * across_plane + me_q, me_n), device_id_type=MESH,
            )

    for load in loads[4:]:
        load.wait()
    present = member[...].astype(F32)
    x, y, z = (coords[r] * present for r in range(3))
    products = [present * present, x * present, y * present, z * present, x * x, y * y, z * z, x * y, x * z, y * z]
    sum_tiles = []
    for base in (0, 8):
        tile = jnp.zeros(shape, F32)
        for q, product in enumerate(products[base : base + 8]):
            tile = jnp.where(row == q, jnp.sum(product, axis=0, keepdims=True), tile)
        for s in (1, 2, 4):
            tile = tile + jnp.where((lane & s) != 0, roll(tile, s, 1), roll(tile, -s, 1))
        sum_tiles.append(tile)
    sums = [sum_tiles[q // 8][q % 8 : q % 8 + 1, :] for q in range(SUMS)]

    def factor(sums):
        n, sx, sy, sz, xx, yy, zz, xy, xz, yz = sums
        l00 = jnp.sqrt(n)
        mx, my, mz = sx / l00, sy / l00, sz / l00
        l33 = jnp.sqrt(xx + yy - mx * mx - my * my)
        l43 = (mx * mz - xz) / l33
        l53 = (my * mz - yz) / l33
        l44 = jnp.sqrt(yy + zz - my * my - mz * mz - l43 * l43)
        l54 = (mx * my - xy - l53 * l43) / l44
        l55 = jnp.sqrt(xx + zz - mx * mx - mz * mz - l53 * l53 - l54 * l54)
        return l00, mx, my, mz, l33, l43, l53, l44, l54, l55

    parts = factor(sums)
    l00, mx, my, mz, l33, l43, l53, l44, l54, l55 = parts
    unit = present / l00
    cx, cy, cz = x - mx * unit, y - my * unit, z - mz * unit
    a0, a1 = -cy / l33, cx / l33
    b0, b1, b2 = -l43 * a0 / l44, (-cz - l43 * a1) / l44, cy / l44
    g0 = (cz - l53 * a0 - l54 * b0) / l55
    g1 = (-l53 * a1 - l54 * b1) / l55
    g2 = (-cx - l54 * b2) / l55
    tent = [unit, a0, a1, b0, b1, b2, g0, g1, g2]
    packl, packr = jnp.zeros(shape, F32), jnp.zeros(shape, F32)
    for j, field in enumerate(tent):
        fields[j] = field
        packl = jnp.where(lane == j, roll(field, j, 1), packl)
        packr = jnp.where(lane == j, roll(field, j + 1, 1), packr)
        tedges[0, j : j + 1, :] = field[:1]
        tedges[1, j : j + 1, :] = field[height - 1 :]
    pack[left] = packl
    pack[right] = packr
    lane_row = lax.broadcasted_iota(jnp.int32, (1, width), 1) % 8
    rows_out = []
    for base in (0, 8):
        line = jnp.zeros((1, width), F32)
        for q, part in enumerate(parts[base : base + 8]):
            line = jnp.where(lane_row == q, part, line)
        rows_out.append(line)
    mine[0:1] = rows_out[0]
    mine[1:2] = rows_out[1]
    gath[me] = jnp.concatenate(rows_out, axis=0)

    def wait_for(code, refs, sem_of):
        @pl.when(present_at[code])
        def _():
            for i, ref in enumerate(refs):
                pltpu.make_async_copy(ref, ref, sem_of(i)).wait()

    tcopies, tarrive = {}, {}
    for code in range(8):
        dy, dx = STEPS[code]
        mine_side, their_side = (left, right) if dx < 0 else (right, left)
        if dx == 0:
            src, dst = tedges.at[0 if dy < 0 else 1], vtrecv.at[1 if dy < 0 else 0]
            arrive = vtrecv.at[0 if dy < 0 else 1]
        elif dy == 0:
            src, dst = pack.at[mine_side], htrecv.at[their_side]
            arrive = htrecv.at[mine_side]
        else:
            edge = 0 if dy < 0 else height - 1
            src = pack.at[mine_side, edge : edge + 1, :]
            dst = ctrecv.at[2 * their_side + (1 if dy < 0 else 0)]
            arrive = ctrecv.at[2 * mine_side + (0 if dy < 0 else 1)]
        copy = pltpu.make_async_remote_copy(
            src_ref=src, dst_ref=dst, send_sem=tsend_sem.at[code], recv_sem=trecv_sem.at[7 - code],
            device_id=target(code), device_id_type=MESH,
        )
        pl.when(present_at[code])(copy.start)
        tcopies[code], tarrive[code] = copy, arrive

    def by_displacement(r0, c0):
        def at(p):
            return ext[p, r0 : r0 + height, c0 : c0 + width]

        for code in range(8):
            masks = [at(codes_at + k) == code for k in range(edge_count)]
            for q in range(9):
                value = jnp.zeros(shape, F32)
                for k in range(edge_count):
                    value = jnp.where(masks[k], at(NB + 9 * k + q), value)
                stencil[code, q, r0 : r0 + height, c0 : c0 + width] = value

    by_displacement(0, 0)

    for code in (3, 4, 0, 2, 5, 7):
        dy, dx = STEPS[code]
        side = right if dx > 0 else left
        ref = wrecv.at[side]
        if dy != 0:
            at = 0 if dy > 0 else ITERS
            ref = wrecv.at[2 + side, :, at : at + ITERS, :]
        wait_for(code, [ref], lambda i, code=code: recv_sem.at[code, i])
    for part, r0 in ((0, 0), (2, height)):
        for p, (t, at, columns) in enumerate(slots):
            from_right = roll(wrecv[part + right, t], -at, 1)
            from_left = roll(wrecv[part + left, t], -at - columns, 1)
            ext[p, r0 : r0 + height, width:] = jnp.where(lane < width // 2, from_right, from_left)
    by_displacement(0, width)
    by_displacement(height, width)

    pl.semaphore_wait(far_sem, plane_count - 1)

    def to_all(src, dst, send, recv):
        def one(i):
            k, n = i // narrow, lax.rem(i, narrow)
            w = jnp.where(2 * me_w < wide, wide - 1 - k, k)
            n = lax.rem(me_n + 1 + n, narrow)

            @pl.when(jnp.logical_or(w != me_w, n != me_n))
            def _():
                pltpu.make_async_remote_copy(
                    src_ref=src, dst_ref=dst, send_sem=send, recv_sem=recv,
                    device_id=(w, n), device_id_type=MESH,
                ).start()

        pl.loop(0, count)(one)

    to_all(mine, gath.at[me], gsend_sem, grecv_sem)

    for code in (1, 6):
        dy, dx = STEPS[code]
        refs = []
        for first, size, deep in ((START, 3, ITERS), (SELF, planes - SELF, ITERS - 1)):
            at = height if dy > 0 else height + 2 * ITERS - deep
            refs.append(ext.at[first : first + size, at : at + deep, 0:width])
        wait_for(code, refs, lambda i, code=code: recv_sem.at[code, i])
    by_displacement(height, 0)

    def full(p):
        return ext[p]

    selfb = {(r, s): (lambda r=r, s=s: ext[SELF + 3 * r + s, 0:height, 0:width]) for r in range(3) for s in range(3)}
    nb = {
        (k, r, s): (lambda k=k, r=r, s=s: ext[NB + 9 * k + 3 * r + s, 0:height, 0:width])
        for k in range(edge_count) for r in range(3) for s in range(3)
    }
    elane = lax.broadcasted_iota(jnp.int32, (2 * height, 2 * width), 1)
    erow = lax.broadcasted_iota(jnp.int32, (2 * height, 2 * width), 0)

    last_row = jnp.where(me_n < narrow - 1, height + ITERS, height)
    back_row = jnp.where(me_n > 0, height + ITERS, 2 * height)
    last_lane = jnp.where(me_w < wide - 1, width + ITERS, width)
    back_lane = jnp.where(me_w > 0, 2 * width - ITERS, 2 * width)
    inside = jnp.logical_and(
        jnp.logical_or(erow < last_row, erow >= back_row), jnp.logical_or(elane < last_lane, elane >= back_lane)
    )
    inverse = [jnp.where(inside, 1.0 / full(SELF + 4 * r), 0.0) for r in range(3)]
    diag = [selfb[r, r]() for r in range(3)]
    inv = [inverse[r][:height, :width] for r in range(3)]

    iterate = [full(START + r) for r in range(3)]
    for number in range(ITERS):
        final = number == ITERS - 1
        rs, cs = (slice(0, height), slice(0, width)) if final else (slice(None), slice(None))
        applied = [sum(ext[SELF + 3 * r + s, rs, cs] * iterate[s][rs, cs] for s in range(3)) for r in range(3)]
        for s in range(3):
            for dx in (-1, 0, 1):
                shifted = roll(iterate[s], -dx, 1)
                for dy in (-1, 0, 1):
                    if (dy, dx) == (0, 0):
                        continue
                    code = STEPS.index((dy, dx))
                    moved = roll(shifted, -dy, 0)[rs, cs]
                    for r in range(3):
                        applied[r] = applied[r] + stencil[code, 3 * r + s, rs, cs] * moved
        mine_it = [v[:height, :width] for v in iterate]
        mine_ap = [v[:height, :width] for v in applied]
        curvature = sum(mine_it[r] * mine_ap[r] for r in range(3))
        energy = sum(mine_it[r] * diag[r] * mine_it[r] for r in range(3))
        partial[number : number + 1] = jnp.sum(curvature, axis=0, keepdims=True)
        partial[number + 4 : number + 5] = jnp.sum(energy, axis=0, keepdims=True)
        iterate = [applied[r] * (inv[r] if final else inverse[r]) for r in range(3)]

    totals = jnp.sum(partial[...], axis=1, keepdims=True)
    line = jnp.sum(jnp.where(lane == row, totals, 0.0), axis=0, keepdims=True)
    sumrow[...] = line
    allsum[me] = line
    to_all(sumrow, allsum.at[me], ssend_sem, srecv_sem)

    for r in range(3):
        iter_ref[r] = iterate[r]

    for code in range(8):
        wait_for(code, [tarrive[code]], lambda i, code=code: trecv_sem.at[code])

    first, last = lane == 0, lane == width - 1
    top, bottom = row == 0, row == height - 1
    lcol, rcol = htrecv[left], htrecv[right]
    corner_l = jnp.where(bottom, ctrecv[2 * left], ctrecv[2 * left + 1])
    corner_r = jnp.where(bottom, ctrecv[2 * right], ctrecv[2 * right + 1])
    for j in range(FIELDS):
        v = tent[j]
        w = jnp.where(bottom, vtrecv[0, j : j + 1, :], vtrecv[1, j : j + 1, :])
        vl = jnp.where(first, roll(lcol, -j, 1), roll(v, 1, 1))
        vr = jnp.where(last, roll(rcol, width - 1 - j, 1), roll(v, -1, 1))
        wl = jnp.where(first, roll(corner_l, -j, 1), roll(w, 1, 1))
        wr = jnp.where(last, roll(corner_r, width - 1 - j, 1), roll(w, -1, 1))
        pairs = ((vl, wl), (v, w), (vr, wr))
        up = [roll(jnp.where(bottom, b, a), 1, 0) for a, b in pairs]
        down = [roll(jnp.where(top, b, a), -1, 0) for a, b in pairs]
        for code, moved in enumerate(up + [vl, vr] + down):
            disp[j, code] = moved

    def piece(block, picked, index):
        unit, a0, a1, b0, b1, b2, g0, g1, g2 = picked
        for r in range(3):
            c0, c1, c2 = (block(r, s) * -inv[r] for s in range(3))
            out_ref[index, 0, r] = c0 * unit
            out_ref[index, 1, r] = c1 * unit
            out_ref[index, 2, r] = c2 * unit
            out_ref[index, 3, r] = c0 * a0 + c1 * a1
            out_ref[index, 4, r] = c0 * b0 + c1 * b1 + c2 * b2
            out_ref[index, 5, r] = c0 * g0 + c1 * g1 + c2 * g2

    piece(lambda r, s: selfb[r, s](), [fields[j] for j in range(FIELDS)], 0)
    for k in range(edge_count):
        masks = [nbr[k] == code for code in range(1, 8)]
        picked = []
        for j in range(FIELDS):
            value = disp[j, 0]
            for code in range(1, 8):
                value = jnp.where(masks[code - 1], disp[j, code], value)
            picked.append(value)
        piece(lambda r, s: nb[k, r, s](), picked, k + 1)

    some = gath.at[pl.ds(0, count - 1)]
    pltpu.make_async_copy(some, some, grecv_sem).wait()
    across = width // TILE * wide
    tiles_x, tiles_y = width // TILE, height // TILE
    crow = lax.broadcasted_iota(jnp.int32, (share, width), 0)
    cgroup = lax.broadcasted_iota(jnp.int32, (share, width), 1) // TILE
    low, high = jnp.zeros((share, width), F32), jnp.zeros((share, width), F32)
    for j in range(share):
        wanted = cmap[me * share + j]
        tile_row, tile_col = wanted // across, lax.rem(wanted, across)
        slot = tile_col // tiles_x * narrow + tile_row // tiles_y
        lines = gath[slot]
        take = jnp.logical_and(crow == j, cgroup == lax.rem(tile_col, tiles_x))
        low = jnp.where(take, lines[0:1], low)
        high = jnp.where(take, lines[1:2], high)
    l00, mx, my, mz, l33, l43, l53, l44, l54, l55 = range(SUMS)
    entries = {
        (0, 0): (l00, 1), (1, 1): (l00, 1), (2, 2): (l00, 1),
        (3, 0): (my, -1), (3, 1): (mx, 1), (4, 1): (mz, -1), (4, 2): (my, 1), (5, 0): (mz, 1), (5, 2): (mx, -1),
        (3, 3): (l33, 1), (4, 3): (l43, 1), (5, 3): (l53, 1), (4, 4): (l44, 1), (5, 4): (l54, 1), (5, 5): (l55, 1),
    }
    outs = coarse_ref.shape[1]
    kind = lax.broadcasted_iota(jnp.int32, (1, outs), 1)
    chosen, sign = jnp.full((1, outs), -1, jnp.int32), jnp.zeros((1, outs), F32)
    for (n, m), (q, way) in entries.items():
        chosen = jnp.where(kind == 6 * m + n, q, chosen)
        sign = jnp.where(kind == 6 * m + n, float(way), sign)
    entry = lax.broadcasted_iota(jnp.int32, (width, outs), 0) % 8
    coarse = jnp.zeros(coarse_ref.shape, F32)
    for base, lines in ((0, low), (8, high)):
        pick = jnp.where(entry + base == chosen, sign, 0.0)
        coarse = coarse + jnp.dot(lines, pick, precision=lax.Precision.HIGHEST, preferred_element_type=F32)
    coarse_ref[...] = coarse

    for code in range(8):
        @pl.when(present_at[code])
        def _(code=code):
            for copy in copies[code] + [tcopies[code]]:
                copy.wait_send()
    for buffer, sem in ((gath, gsend_sem), (allsum, ssend_sem)):
        some = buffer.at[pl.ds(0, count - 1)]
        pltpu.make_async_copy(some, some, sem).wait()

    some = allsum.at[pl.ds(0, count - 1)]
    pltpu.make_async_copy(some, some, srecv_sem).wait()
    if count <= 64:
        lines = [allsum[d] for d in range(count)]
        while len(lines) > 1:
            lines = [a + b for a, b in zip(lines[::2], lines[1::2])] + ([lines[-1]] if len(lines) % 2 else [])
        total = lines[0]
    else:
        total = lax.fori_loop(0, count, lambda d, t: t + allsum[d], jnp.zeros((1, width), F32))
    values = [jnp.broadcast_to(total[:, i : i + 1], shape) for i in range(2 * ITERS)]
    ratios = [values[i + ITERS] / values[i] for i in range(ITERS)]
    growth = ratios[0]
    for i in range(1, ITERS):
        growth = growth * ratios[i]
    scale_ref[0] = ratios[ITERS - 1] * (4.0 / 3.0)
    scale_ref[1] = growth


def finish(raw, fields, iterate, scale, coarse, out_h, probe_h, coarse_h, out, probe, sem):
    weight = scale[0]
    base = {(0, 0): 0, (1, 1): 0, (2, 2): 0, (3, 0): 1, (3, 1): 2}
    for r in range(3):
        base[(4, r)] = 3 + r
        base[(5, r)] = 6 + r
    blocks, modes = raw.shape[:2]
    last = pltpu.make_async_copy(coarse, coarse_h, sem.at[blocks + 1])
    last.start()
    copies = [last]
    for k in range(blocks):
        for m in range(modes):
            for r in range(3):
                value = raw[k, m, r] * weight
                out[k, m, r] = value + fields[base[(m, r)]] if k == 0 and (m, r) in base else value
        copy = pltpu.make_async_copy(out.at[k], out_h.at[k], sem.at[k])
        copy.start()
        copies.append(copy)
    for r in range(3):
        probe[r] = iterate[r] * scale[1]
    copy = pltpu.make_async_copy(probe, probe_h, sem.at[blocks])
    copy.start()
    copies.append(copy)
    for copy in copies:
        copy.wait()


def local(wide, narrow, coords, member, start_vector, self_block, neighbour_block, neighbours, coarse_map):
    height, width = member.shape
    edge_count = neighbours.shape[0]
    count = wide * narrow
    share = coarse_map.shape[0] // count
    tile = (height, width)
    double = (2 * height, 2 * width)
    planes = 12 + 10 * edge_count
    tiles = edge_slots(planes, width)[1]
    vmem = pltpu.VMEM
    dma = pltpu.SemaphoreType.DMA
    results = (
        jax.ShapeDtypeStruct((edge_count + 1, 6, 3) + tile, F32),
        jax.ShapeDtypeStruct((3,) + tile, F32),
        jax.ShapeDtypeStruct((share, 36), F32),
    )
    staged = pl.pallas_call(
        functools.partial(kernel, wide, narrow, share),
        out_shape=(
            results[0],
            jax.ShapeDtypeStruct((FIELDS,) + tile, F32),
            results[1],
            jax.ShapeDtypeStruct((2,) + tile, F32),
            results[2],
        ),
        in_specs=[pl.BlockSpec(memory_space=pl.ANY)] * 7,
        out_specs=(pl.BlockSpec(memory_space=pltpu.VMEM),) * 5,
        scratch_shapes=[
            vmem((3,) + tile, F32),
            vmem(tile, jnp.int32),
            vmem((edge_count,) + tile, jnp.int32),
            pltpu.SMEM(coarse_map.shape, jnp.int32),
            vmem((planes,) + double, F32),
            vmem((2, tiles) + tile, F32),
            vmem((8, 9) + double, F32),
            vmem((2,) + tile, F32),
            vmem((2, 16, width), F32),
            vmem((FIELDS, 8) + tile, F32),
            vmem((2, width), F32),
            vmem((count, 2, width), F32),
            vmem((1, width), F32),
            vmem((count, 1, width), F32),
            vmem((8, width), F32),
            vmem((4, tiles) + tile, F32),
            vmem((2,) + tile, F32),
            vmem((2, 16, width), F32),
            vmem((4, 1, width), F32),
            dma((7,)),
            dma((8, 2)),
            dma((8, 2)),
            dma((8,)),
            dma((8,)),
            dma(()),
            dma(()),
            dma(()),
            dma(()),
            pltpu.SemaphoreType.REGULAR,
        ],
        compiler_params=pltpu.CompilerParams(collective_id=0, has_side_effects=True, vmem_limit_bytes=VMEM_LIMIT),
    )(*(
        pltpu.with_memory_space_constraint(value, pltpu.HBM)
        for value in (
            coords, member, start_vector, self_block.reshape((9,) + tile), neighbour_block.reshape((-1,) + tile),
            neighbours, coarse_map,
        )
    ))
    smoothed, probe, coarse = pl.pallas_call(
        finish,
        out_shape=results,
        in_specs=[pl.BlockSpec(memory_space=pltpu.VMEM)] * 5,
        out_specs=(pl.BlockSpec(memory_space=pl.ANY),) * 3,
        scratch_shapes=[
            vmem(results[0].shape, F32),
            vmem(results[1].shape, F32),
            dma((edge_count + 3,)),
        ],
        compiler_params=pltpu.CompilerParams(vmem_limit_bytes=VMEM_LIMIT),
    )(*staged)
    return smoothed, probe, coarse.T


def solution(mesh):
    return jax.shard_map(
        functools.partial(local, mesh.shape["wide"], mesh.shape["narrow"]),
        mesh=mesh,
        in_specs=(
            P(None, "narrow", "wide"),
            P("narrow", "wide"),
            P(None, "narrow", "wide"),
            P(None, None, "narrow", "wide"),
            P(None, None, None, "narrow", "wide"),
            P(None, "narrow", "wide"),
            P(),
        ),
        out_specs=(
            P(None, None, None, "narrow", "wide"),
            P(None, "narrow", "wide"),
            P(None, ("wide", "narrow")),
        ),
        check_vma=False,
    )
```

time: 23.3 us -> 18.3 us (0.79)
  local copies, waits for them, and re-layouts: 3.17 us -> 0 us
  Pallas kernels: 19.2 us -> 17.5 us
    unnamed x7 -> x0, local copies, waits for them, and re-layouts: 3.17 us -> none
    pallas_call x1, Pallas kernels: 19.2 us -> 16.6 us  [local(): pl.pallas_call(functools.partial(kernel, wide, narrow, share), out_shape=...]
    pallas_call x0 -> x1, Pallas kernels: none -> 0.87 us  [local(): pl.pallas_call(finish, out_shape=results, in_specs=[pl.BlockSpec(memory_s...]
where the time goes in v1:
time: 18.3 us; the launch traced here: 18.1 us
  Pallas kernels  17.5 us (96%)
  between operations  0.64 us (3%)
    pallas_call x1, Pallas kernels, local(): pl.pallas_call(functools.partial(kernel, wide, narrow, share), out_shape=...  16.6 us
    pallas_call x1, Pallas kernels, local(): pl.pallas_call(finish, out_shape=results, in_specs=[pl.BlockSpec(memory_s...  0.87 us

profile of v1, /device:TPU:0, one launch (start us, length us, event | category | flops | bytes accessed | tf_op | source)
XLA Modules:
  0.0 18.1 jit_solution(11634529998647153602)
XLA Ops:
  0.6 16.6 %shard_map.94 = (f32[7,6,3,8,128]{4,3,2,1,0:T(8,128)S(1)}, f32[9,8,128]{2,1,0:T(8,128)S(1)}, f32[3,8,128]{2,1,0:T(8,128)S(1)}, f32[2,8,128]{2,1,0:T(8,128)S(1)}, f32[16,36]{1,0:T(8,128)S(1)}) custom-call(f32[3,8,128]{2,1,0:T(8,128)} %coords_h.1, s32[8,128]{1,0:T(8,128)} %member_h.1, f32[3,8,128]{2,1,0:T(8,128)} %start_h.1, f32[9,8,128]{2,1,0:T(8,128)} %bitcast.4, ...), custom_call_target="tpu_custom_call" | custom-call | tf_op jit(solution)/shard_map/pallas_call | solution.py:543
  17.3 0.9 %shard_map.95 = (f32[7,6,3,8,128]{4,3,2,1,0:T(8,128)}, f32[3,8,128]{2,1,0:T(8,128)}, f32[16,36]{1,0:T(8,128)}) custom-call(f32[7,6,3,8,128]{4,3,2,1,0:T(8,128)S(1)} %get-tuple-element.11.raw, f32[9,8,128]{2,1,0:T(8,128)S(1)} %get-tuple-element.12.fields, f32[3,8,128]{2,1,0:T(8,128)S(1)} %get-tuple-element.13.iterate, ...), custom_call_target="tpu_custom_call" | custom-call | tf_op jit(solution)/shard_map/pallas_call | solution.py:593

commit v2 on v1

--- a/solution.py
+++ b/solution.py
@@ -30,14 +30,23 @@
 
 
 def edge_slots(planes, width):
-    slots, tile, at = [], 0, 0
-    for p in range(planes):
-        columns = ITERS if p < SELF else ITERS - 1
-        if at + columns > width:
-            tile, at = tile + 1, 0
-        slots.append((tile, at, columns))
-        at += columns
-    return slots, tile + 1
+    per = width // (ITERS - 1)
+    tiles = pl.cdiv(planes - SELF, per)
+    slots = [(tiles, ITERS * p, ITERS) for p in range(SELF)]
+    slots += [(p // per, p % per * (ITERS - 1), ITERS - 1) for p in range(planes - SELF)]
+    return slots, tiles
+
+
+def rounds_of(across_plane, narrow):
+    offsets, reach = [1], 1
+    while reach < max(across_plane, narrow) - 1:
+        offsets.append(reach + 1)
+        reach = 2 * reach + 1
+    return offsets
+
+
+IN_ROWS, IN_COORDS, IN_MAP = range(3)
+SIDES, CORNERS, STARTS, BANDS, EDGES, GATHER, TOTALS = range(7)
 
 
 def kernel(
@@ -46,8 +55,8 @@
     out_ref, fields, iter_ref, scale_ref, coarse_ref,
     coords, member, nbr, cmap,
     ext, wpack, stencil, pack, tedges, disp, mine, gath, sumrow, allsum, partial,
-    wrecv, htrecv, vtrecv, ctrecv,
-    in_sem, send_sem, recv_sem, tsend_sem, trecv_sem, gsend_sem, grecv_sem, ssend_sem, srecv_sem, far_sem,
+    wrecv, htrecv, vtrecv, ctrecv, firsts_own, firsts,
+    tally, in_sem, send_sem, recv_sem, round_sem,
 ):
     count = wide * narrow
     me_w, me_n = lax.axis_index("wide"), lax.axis_index("narrow")
@@ -62,6 +71,7 @@
     codes_at = NB + 9 * edge_count
     planes = codes_at + edge_count
     slots, tiles = edge_slots(planes, width)
+    offsets = rounds_of(across_plane, narrow)
     right, left = 0, 1
 
     def exists(code):
@@ -86,7 +96,7 @@
         return cond.astype(jnp.int32)
 
     expected = 0
-    for code in (1, 6, 0, 2, 5, 7, 3, 4):
+    for code in (1, 6):
         expected = expected + greet(present_at[code], target(code))
 
     def own(first, size):
@@ -94,26 +104,60 @@
 
     loads = [
         pltpu.make_async_copy(src, dst, in_sem.at[i])
-        for i, (src, dst) in enumerate(
-            (
-                (nbr_h, nbr), (start_h, own(START, 3)), (self_h, own(SELF, 9)), (nb_h, own(NB, nb_h.shape[0])),
-                (coords_h, coords), (member_h, member), (cmap_h, cmap),
-            )
+        for src, dst, i in (
+            (nb_h, own(NB, nb_h.shape[0]), IN_ROWS), (self_h, own(SELF, 9), IN_ROWS), (start_h, own(START, 3), IN_ROWS),
+            (nbr_h, nbr, IN_ROWS), (coords_h, coords, IN_COORDS), (member_h, member, IN_COORDS), (cmap_h, cmap, IN_MAP),
         )
     ]
     for load in loads:
         load.start()
 
-    def near(w, n):
-        return jnp.logical_and(jnp.abs(w - me_w) <= 1, jnp.abs(n - me_n) <= 1)
-
-    for q in range(across_plane):
-        for n in range(narrow):
-            w = me_p * across_plane + q
-            expected = expected + greet(jnp.logical_not(near(w, n)), (w, n))
+    def wait_rows(sem, rows):
+        some = tally.at[0:rows]
+        pltpu.make_async_copy(some, some, sem).wait()
+
+    sides_here = (me_w > 0).astype(jnp.int32) + (me_w < wide - 1).astype(jnp.int32)
+    ends_here = (me_n > 0).astype(jnp.int32) + (me_n < narrow - 1).astype(jnp.int32)
+
+    def wait_halo(sem, side, end, corner, more=0):
+        for a in range(min(wide - 1, 1), min(wide - 1, 2) + 1):
+            for b in range(min(narrow - 1, 1), min(narrow - 1, 2) + 1):
+                rows = a * side + b * end + a * b * corner + more
+                if rows:
+                    pl.when(jnp.logical_and(sides_here == a, ends_here == b))(functools.partial(wait_rows, sem, rows))
+
+    for code in (0, 2, 5, 7, 3, 4):
+        expected = expected + greet(present_at[code], target(code))
+
     for p in range(plane_count):
         w = p * across_plane + me_q
-        expected = expected + greet(jnp.logical_and(p != me_p, jnp.logical_not(near(w, me_n))), (w, me_n))
+        expected = expected + greet(jnp.abs(w - me_w) > 1, (w, me_n))
+
+    def partners(offset):
+        for dq in (-offset, 0, offset):
+            for dn in (-offset, 0, offset):
+                if (dq, dn) != (0, 0) and abs(dq) < across_plane and abs(dn) < narrow:
+                    q, n = me_q + dq, me_n + dn
+                    fits = [cond for step, cond in (
+                        (-dq, q >= 0), (dq, q < across_plane), (-dn, n >= 0), (dn, n < narrow),
+                    ) if step > 0]
+                    yield functools.reduce(jnp.logical_and, fits), (me_w + dq, n)
+
+    def tell(number):
+        for cond, device in partners(offsets[number]):
+            @pl.when(cond)
+            def _(device=device):
+                pl.semaphore_signal(round_sem.at[number], inc=1, device_id=device, device_id_type=MESH)
+
+    def hear(number):
+        pl.semaphore_wait(round_sem.at[number], sum(cond.astype(jnp.int32) for cond, _ in partners(offsets[number])))
+
+    deep = ITERS - 1
+
+    def corner_refs(ref, low):
+        at = 0 if low else height - deep
+        start_at = 0 if low else height - ITERS
+        return [ref.at[0:tiles, at : at + deep, :], ref.at[tiles, start_at : start_at + ITERS, :]]
 
     for code in range(8):
         dy, dx = STEPS[code]
@@ -124,80 +168,127 @@
                 at = height if dy > 0 else height + ITERS
                 ext[:, at : at + ITERS, 0:width] = jnp.zeros((planes, ITERS, width), F32)
                 vtrecv[0 if dy < 0 else 1] = jnp.zeros(vtrecv.shape[1:], F32)
+                at = deep - 1 if dy > 0 else height - deep
+                firsts[:, at : at + 1, :] = jnp.zeros((3, 1, width), F32)
+                at = deep if dy > 0 else height - deep - 1
+                for to in (right, left):
+                    wrecv[2 + to, 0:tiles, at : at + 1, :] = jnp.zeros((tiles, 1, width), F32)
             elif dy == 0:
                 wrecv[side] = jnp.zeros(wrecv.shape[1:], F32)
                 htrecv[side] = jnp.zeros(htrecv.shape[1:], F32)
             else:
-                at = 0 if dy > 0 else ITERS
-                wrecv[2 + side, :, at : at + ITERS, :] = jnp.zeros((tiles, ITERS, width), F32)
+                for ref in corner_refs(wrecv.at[2 + side], dy > 0):
+                    ref[...] = jnp.zeros(ref.shape, F32)
                 ctrecv[2 * side + (0 if dy < 0 else 1)] = jnp.zeros(ctrecv.shape[1:], F32)
 
     lane = lax.broadcasted_iota(jnp.int32, shape, 1)
     row = lax.broadcasted_iota(jnp.int32, shape, 0)
-
-    for load in loads[:4]:
-        load.wait()
+    first, last = lane == 0, lane == width - 1
+
+    wait_rows(in_sem.at[IN_ROWS], planes * height)
     for k in range(edge_count):
         ext[codes_at + k, 0:height, 0:width] = nbr[k].astype(F32)
-    for side in (right, left):
-        packed = [jnp.zeros(shape, F32) for _ in range(tiles)]
-        for p, (t, at, columns) in enumerate(slots):
-            first = 0 if side == left else width - columns
-            moved = roll(ext[p, 0:height, 0:width], at - first, 1)
-            packed[t] = moved if at == 0 else jnp.where(lane >= at, moved, packed[t])
-        for t in range(tiles):
-            wpack[side, t] = packed[t]
 
     pl.semaphore_wait(barrier, expected)
-
-    pieces_of = {}
-    for code in range(8):
-        dy, dx = STEPS[code]
-        if dx == 0:
-            pairs = []
-            for first, size, deep in ((START, 3, ITERS), (SELF, planes - SELF, ITERS - 1)):
-                here = 0 if dy < 0 else height - deep
-                there = height if dy < 0 else height + 2 * ITERS - deep
-                pairs.append((
-                    ext.at[first : first + size, here : here + deep, 0:width],
-                    ext.at[first : first + size, there : there + deep, 0:width],
-                ))
-        else:
-            mine_side, their_side = (left, right) if dx < 0 else (right, left)
-            if dy == 0:
-                pairs = [(wpack.at[mine_side], wrecv.at[their_side])]
-            else:
-                at = 0 if dy < 0 else ITERS
-                pairs = [(
-                    wpack.at[mine_side, :, at : at + ITERS, :], wrecv.at[2 + their_side, :, at : at + ITERS, :],
-                )]
-        pieces_of[code] = pairs
-
-    copies = {}
-    for code in (1, 6, 0, 2, 5, 7, 3, 4):
+    tell(0)
+
+    def send(code, pairs, group):
         made = [
             pltpu.make_async_remote_copy(
-                src_ref=src, dst_ref=dst, send_sem=send_sem.at[code, i], recv_sem=recv_sem.at[7 - code, i],
+                src_ref=src, dst_ref=dst, send_sem=send_sem, recv_sem=recv_sem.at[group],
                 device_id=target(code), device_id_type=MESH,
             )
-            for i, (src, dst) in enumerate(pieces_of[code])
+            for src, dst in pairs
         ]
 
         @pl.when(present_at[code])
-        def _(made=made):
+        def _():
             for copy in made:
                 copy.start()
-        copies[code] = made
-
-    for p in range(plane_count):
-        @pl.when(p != me_p)
-        def _(p=p):
-            pl.semaphore_signal(
-                far_sem, inc=1, device_id=(p * across_plane + me_q, me_n), device_id_type=MESH,
-            )
-
-    for load in loads[4:]:
-        load.wait()
+
+    bands = ((START, 3, ITERS), (SELF, 9, deep - 1), (NB, planes - NB, deep - 1))
+
+    def band_pairs(code, band):
+        base, size, rows = band
+        here, there = (0, height) if STEPS[code][0] < 0 else (height - rows, height + 2 * ITERS - rows)
+        return [(
+            ext.at[base : base + size, here : here + rows, 0:width],
+            ext.at[base : base + size, there : there + rows, 0:width],
+        )]
+
+    def end_pairs(code):
+        here, there = (deep - 1, deep) if STEPS[code][0] < 0 else (height - deep, height - deep - 1)
+        return [
+            (wpack.at[side, 0:tiles, here : here + 1, :], wrecv.at[3 - side, 0:tiles, there : there + 1, :])
+            for side in (right, left)
+        ]
+
+    def first_pairs(code):
+        here = deep - 1 if STEPS[code][0] < 0 else height - deep
+        return [(firsts_own.at[:, here : here + 1, :], firsts.at[:, here : here + 1, :])]
+
+    for code in (1, 6):
+        send(code, band_pairs(code, bands[0]), STARTS)
+        send(code, band_pairs(code, bands[1]), BANDS)
+    for side in (right, left):
+        packed = [jnp.zeros(shape, F32) for _ in range(tiles + 1)]
+        for p, (t, at, columns) in enumerate(slots):
+            begin = 0 if side == left else width - columns
+            moved = roll(ext[p, 0:height, 0:width], at - begin, 1)
+            packed[t] = moved if at == 0 else jnp.where(lane >= at, moved, packed[t])
+        for t in range(tiles + 1):
+            wpack[side, t] = packed[t]
+
+    for code in (0, 2, 5, 7, 3, 4):
+        dy, dx = STEPS[code]
+        mine_side, their_side = (left, right) if dx < 0 else (right, left)
+        if dy == 0:
+            send(code, [(wpack.at[mine_side], wrecv.at[their_side])], SIDES)
+        else:
+            send(code, list(zip(
+                corner_refs(wpack.at[mine_side], dy < 0), corner_refs(wrecv.at[2 + their_side], dy < 0),
+            )), CORNERS)
+    for code in (1, 6):
+        send(code, end_pairs(code), CORNERS)
+        send(code, band_pairs(code, bands[2]), BANDS)
+
+    def by_displacement(r0, c0):
+        def at(p):
+            return ext[p, r0 : r0 + height, c0 : c0 + width]
+
+        for group in range(0, 8, 2):
+            masks = {(code, k): at(codes_at + k) == code for code in (group, group + 1) for k in range(edge_count)}
+            for q in range(9):
+                blocks = [at(NB + 9 * k + q) for k in range(edge_count)]
+                for code in (group, group + 1):
+                    value = jnp.zeros(shape, F32)
+                    for k in range(edge_count):
+                        value = jnp.where(masks[code, k], blocks[k], value)
+                    stencil[code, q, r0 : r0 + height, c0 : c0 + width] = value
+
+    def apply(iterate, rs, cs):
+        applied = [sum(ext[SELF + 3 * r + s, rs, cs] * iterate[s][rs, cs] for s in range(3)) for r in range(3)]
+        for s in range(3):
+            for dx in (0, -1, 1):
+                shifted = roll(iterate[s], -dx, 1)
+                for dy in (-1, 0, 1):
+                    if (dy, dx) == (0, 0):
+                        continue
+                    code = STEPS.index((dy, dx))
+                    moved = roll(shifted, -dy, 0)[rs, cs]
+                    for r in range(3):
+                        applied[r] = applied[r] + stencil[code, 3 * r + s, rs, cs] * moved
+        return applied
+
+    by_displacement(0, 0)
+    inside_rows, inside_cols = slice(0, height), slice(0, width)
+    applied = apply([ext[START + r, 0:height, 0:width] for r in range(3)], inside_rows, inside_cols)
+    for r in range(3):
+        firsts_own[r] = applied[r] * (1.0 / ext[SELF + 4 * r, 0:height, 0:width])
+    for code in (1, 6):
+        send(code, first_pairs(code), BANDS)
+
+    wait_rows(in_sem.at[IN_COORDS], 4 * height)
     present = member[...].astype(F32)
     x, y, z = (coords[r] * present for r in range(3))
     products = [present * present, x * present, y * present, z * present, x * x, y * y, z * z, x * y, x * z, y * z]
@@ -238,8 +329,8 @@
         fields[j] = field
         packl = jnp.where(lane == j, roll(field, j, 1), packl)
         packr = jnp.where(lane == j, roll(field, j + 1, 1), packr)
-        tedges[0, j : j + 1, :] = field[:1]
-        tedges[1, j : j + 1, :] = field[height - 1 :]
+        tedges[0, j] = field[:1]
+        tedges[1, j] = field[height - 1 :]
     pack[left] = packl
     pack[right] = packr
     lane_row = lax.broadcasted_iota(jnp.int32, (1, width), 1) % 8
@@ -253,90 +344,72 @@
     mine[1:2] = rows_out[1]
     gath[me] = jnp.concatenate(rows_out, axis=0)
 
-    def wait_for(code, refs, sem_of):
-        @pl.when(present_at[code])
-        def _():
-            for i, ref in enumerate(refs):
-                pltpu.make_async_copy(ref, ref, sem_of(i)).wait()
-
-    tcopies, tarrive = {}, {}
     for code in range(8):
         dy, dx = STEPS[code]
         mine_side, their_side = (left, right) if dx < 0 else (right, left)
         if dx == 0:
             src, dst = tedges.at[0 if dy < 0 else 1], vtrecv.at[1 if dy < 0 else 0]
-            arrive = vtrecv.at[0 if dy < 0 else 1]
         elif dy == 0:
             src, dst = pack.at[mine_side], htrecv.at[their_side]
-            arrive = htrecv.at[mine_side]
         else:
             edge = 0 if dy < 0 else height - 1
             src = pack.at[mine_side, edge : edge + 1, :]
             dst = ctrecv.at[2 * their_side + (1 if dy < 0 else 0)]
-            arrive = ctrecv.at[2 * mine_side + (0 if dy < 0 else 1)]
-        copy = pltpu.make_async_remote_copy(
-            src_ref=src, dst_ref=dst, send_sem=tsend_sem.at[code], recv_sem=trecv_sem.at[7 - code],
-            device_id=target(code), device_id_type=MESH,
-        )
-        pl.when(present_at[code])(copy.start)
-        tcopies[code], tarrive[code] = copy, arrive
-
-    def by_displacement(r0, c0):
-        def at(p):
-            return ext[p, r0 : r0 + height, c0 : c0 + width]
-
-        for code in range(8):
-            masks = [at(codes_at + k) == code for k in range(edge_count)]
-            for q in range(9):
-                value = jnp.zeros(shape, F32)
-                for k in range(edge_count):
-                    value = jnp.where(masks[k], at(NB + 9 * k + q), value)
-                stencil[code, q, r0 : r0 + height, c0 : c0 + width] = value
-
-    by_displacement(0, 0)
-
-    for code in (3, 4, 0, 2, 5, 7):
-        dy, dx = STEPS[code]
-        side = right if dx > 0 else left
-        ref = wrecv.at[side]
-        if dy != 0:
-            at = 0 if dy > 0 else ITERS
-            ref = wrecv.at[2 + side, :, at : at + ITERS, :]
-        wait_for(code, [ref], lambda i, code=code: recv_sem.at[code, i])
-    for part, r0 in ((0, 0), (2, height)):
+        send(code, [(src, dst)], EDGES)
+
+    for number in range(len(offsets) - 1):
+        hear(number)
+        tell(number + 1)
+    def unpack(part, r0):
         for p, (t, at, columns) in enumerate(slots):
             from_right = roll(wrecv[part + right, t], -at, 1)
             from_left = roll(wrecv[part + left, t], -at - columns, 1)
-            ext[p, r0 : r0 + height, width:] = jnp.where(lane < width // 2, from_right, from_left)
+            both = jnp.where(lane < width // 2, from_right, from_left)
+            ext[p, r0 : r0 + height, width:] = both
+            if part and p >= SELF:
+                ext[p, height + deep - 1 : height + deep, 0:width] = both[deep : deep + 1]
+                ext[p, 2 * height - deep : 2 * height - deep + 1, 0:width] = both[height - deep - 1 : height - deep]
+
+    side_rows, start_rows = (tiles + 1) * height, SELF * ITERS
+    corner_rows, end_rows = tiles * deep + ITERS, 2 * tiles
+    band_rows = (planes - SELF) * (deep - 1) + 3
+    edge_rows = (height, FIELDS, 1)
+    wait_halo(recv_sem.at[SIDES], side_rows, 0, 0)
+    unpack(0, 0)
     by_displacement(0, width)
-    by_displacement(height, width)
-
-    pl.semaphore_wait(far_sem, plane_count - 1)
-
-    def to_all(src, dst, send, recv):
+
+    hear(len(offsets) - 1)
+
+    def to_all(src, dst, group):
         def one(i):
-            k, n = i // narrow, lax.rem(i, narrow)
+            k = i // narrow
             w = jnp.where(2 * me_w < wide, wide - 1 - k, k)
-            n = lax.rem(me_n + 1 + n, narrow)
+            n = lax.rem(me_n + 1 + i, narrow)
 
             @pl.when(jnp.logical_or(w != me_w, n != me_n))
             def _():
                 pltpu.make_async_remote_copy(
-                    src_ref=src, dst_ref=dst, send_sem=send, recv_sem=recv,
+                    src_ref=src, dst_ref=dst, send_sem=send_sem, recv_sem=recv_sem.at[group],
                     device_id=(w, n), device_id_type=MESH,
                 ).start()
 
-        pl.loop(0, count)(one)
-
-    to_all(mine, gath.at[me], gsend_sem, grecv_sem)
-
-    for code in (1, 6):
-        dy, dx = STEPS[code]
-        refs = []
-        for first, size, deep in ((START, 3, ITERS), (SELF, planes - SELF, ITERS - 1)):
-            at = height if dy > 0 else height + 2 * ITERS - deep
-            refs.append(ext.at[first : first + size, at : at + deep, 0:width])
-        wait_for(code, refs, lambda i, code=code: recv_sem.at[code, i])
+        if count <= 64:
+            for i in range(count):
+                one(i)
+        else:
+            pl.loop(0, count)(one)
+
+    to_all(mine, gath.at[me], GATHER)
+
+    wait_halo(recv_sem.at[CORNERS], 0, end_rows, corner_rows)
+    unpack(2, height)
+    by_displacement(height, width)
+    wait_halo(recv_sem.at[STARTS], 0, start_rows, 0)
+    whole_cols, beyond = slice(None), slice(width, None)
+    begin = [ext[START + r] for r in range(3)]
+    begin_top = apply(begin, inside_rows, whole_cols)
+    begin_corner = apply(begin, slice(height, None), beyond)
+    wait_halo(recv_sem.at[BANDS], 0, band_rows, 0)
     by_displacement(height, 0)
 
     def full(p):
@@ -361,21 +434,24 @@
     diag = [selfb[r, r]() for r in range(3)]
     inv = [inverse[r][:height, :width] for r in range(3)]
 
-    iterate = [full(START + r) for r in range(3)]
+    sent = jnp.logical_and(
+        jnp.logical_or(erow == height + deep - 1, erow == 2 * height - deep),
+        jnp.logical_and(elane > 0, elane < width - 1),
+    )
+    spread = [
+        jnp.concatenate([jnp.concatenate([firsts[r], firsts[r]], axis=0)] * 2, axis=1) for r in range(3)
+    ]
+    iterate = begin
     for number in range(ITERS):
         final = number == ITERS - 1
         rs, cs = (slice(0, height), slice(0, width)) if final else (slice(None), slice(None))
-        applied = [sum(ext[SELF + 3 * r + s, rs, cs] * iterate[s][rs, cs] for s in range(3)) for r in range(3)]
-        for s in range(3):
-            for dx in (-1, 0, 1):
-                shifted = roll(iterate[s], -dx, 1)
-                for dy in (-1, 0, 1):
-                    if (dy, dx) == (0, 0):
-                        continue
-                    code = STEPS.index((dy, dx))
-                    moved = roll(shifted, -dy, 0)[rs, cs]
-                    for r in range(3):
-                        applied[r] = applied[r] + stencil[code, 3 * r + s, rs, cs] * moved
+        if number == 0:
+            outer = apply(begin, slice(height, None), inside_cols)
+            applied = [
+                jnp.concatenate([begin_top[r], jnp.concatenate([outer[r], begin_corner[r]], axis=1)], axis=0) for r in range(3)
+            ]
+        else:
+            applied = apply(iterate, rs, cs)
         mine_it = [v[:height, :width] for v in iterate]
         mine_ap = [v[:height, :width] for v in applied]
         curvature = sum(mine_it[r] * mine_ap[r] for r in range(3))
@@ -383,27 +459,27 @@
         partial[number : number + 1] = jnp.sum(curvature, axis=0, keepdims=True)
         partial[number + 4 : number + 5] = jnp.sum(energy, axis=0, keepdims=True)
         iterate = [applied[r] * (inv[r] if final else inverse[r]) for r in range(3)]
+        if number == 0:
+            iterate = [jnp.where(sent, spread[r], iterate[r]) for r in range(3)]
 
     totals = jnp.sum(partial[...], axis=1, keepdims=True)
     line = jnp.sum(jnp.where(lane == row, totals, 0.0), axis=0, keepdims=True)
     sumrow[...] = line
     allsum[me] = line
-    to_all(sumrow, allsum.at[me], ssend_sem, srecv_sem)
+    to_all(sumrow, allsum.at[me], TOTALS)
 
     for r in range(3):
         iter_ref[r] = iterate[r]
 
-    for code in range(8):
-        wait_for(code, [tarrive[code]], lambda i, code=code: trecv_sem.at[code])
-
-    first, last = lane == 0, lane == width - 1
+    wait_halo(recv_sem.at[EDGES], *edge_rows)
+
     top, bottom = row == 0, row == height - 1
     lcol, rcol = htrecv[left], htrecv[right]
     corner_l = jnp.where(bottom, ctrecv[2 * left], ctrecv[2 * left + 1])
     corner_r = jnp.where(bottom, ctrecv[2 * right], ctrecv[2 * right + 1])
     for j in range(FIELDS):
         v = tent[j]
-        w = jnp.where(bottom, vtrecv[0, j : j + 1, :], vtrecv[1, j : j + 1, :])
+        w = jnp.where(bottom, vtrecv[0, j], vtrecv[1, j])
         vl = jnp.where(first, roll(lcol, -j, 1), roll(v, 1, 1))
         vr = jnp.where(last, roll(rcol, width - 1 - j, 1), roll(v, -1, 1))
         wl = jnp.where(first, roll(corner_l, -j, 1), roll(w, 1, 1))
@@ -436,8 +512,9 @@
             picked.append(value)
         piece(lambda r, s: nb[k, r, s](), picked, k + 1)
 
+    loads[6].wait()
     some = gath.at[pl.ds(0, count - 1)]
-    pltpu.make_async_copy(some, some, grecv_sem).wait()
+    pltpu.make_async_copy(some, some, recv_sem.at[GATHER]).wait()
     across = width // TILE * wide
     tiles_x, tiles_y = width // TILE, height // TILE
     crow = lax.broadcasted_iota(jnp.int32, (share, width), 0)
@@ -470,17 +547,13 @@
         coarse = coarse + jnp.dot(lines, pick, precision=lax.Precision.HIGHEST, preferred_element_type=F32)
     coarse_ref[...] = coarse
 
-    for code in range(8):
-        @pl.when(present_at[code])
-        def _(code=code):
-            for copy in copies[code] + [tcopies[code]]:
-                copy.wait_send()
-    for buffer, sem in ((gath, gsend_sem), (allsum, ssend_sem)):
-        some = buffer.at[pl.ds(0, count - 1)]
-        pltpu.make_async_copy(some, some, sem).wait()
+    wait_halo(
+        send_sem, side_rows + edge_rows[0], end_rows + start_rows + band_rows + edge_rows[1], corner_rows + edge_rows[2],
+        3 * (count - 1),
+    )
 
     some = allsum.at[pl.ds(0, count - 1)]
-    pltpu.make_async_copy(some, some, srecv_sem).wait()
+    pltpu.make_async_copy(some, some, recv_sem.at[TOTALS]).wait()
     if count <= 64:
         lines = [allsum[d] for d in range(count)]
         while len(lines) > 1:
@@ -504,23 +577,18 @@
         base[(4, r)] = 3 + r
         base[(5, r)] = 6 + r
     blocks, modes = raw.shape[:2]
-    last = pltpu.make_async_copy(coarse, coarse_h, sem.at[blocks + 1])
-    last.start()
-    copies = [last]
+    small = [pltpu.make_async_copy(coarse, coarse_h, sem.at[1]), pltpu.make_async_copy(probe, probe_h, sem.at[2])]
+    small[0].start()
     for k in range(blocks):
         for m in range(modes):
             for r in range(3):
                 value = raw[k, m, r] * weight
                 out[k, m, r] = value + fields[base[(m, r)]] if k == 0 and (m, r) in base else value
-        copy = pltpu.make_async_copy(out.at[k], out_h.at[k], sem.at[k])
-        copy.start()
-        copies.append(copy)
+        pltpu.make_async_copy(out.at[k], out_h.at[k], sem.at[0]).start()
     for r in range(3):
         probe[r] = iterate[r] * scale[1]
-    copy = pltpu.make_async_copy(probe, probe_h, sem.at[blocks])
-    copy.start()
-    copies.append(copy)
-    for copy in copies:
+    small[1].start()
+    for copy in small + [pltpu.make_async_copy(out, out_h, sem.at[0])]:
         copy.wait()
 
 
@@ -532,7 +600,7 @@
     tile = (height, width)
     double = (2 * height, 2 * width)
     planes = 12 + 10 * edge_count
-    tiles = edge_slots(planes, width)[1]
+    tiles = edge_slots(planes, width)[1] + 1
     vmem = pltpu.VMEM
     dma = pltpu.SemaphoreType.DMA
     results = (
@@ -560,7 +628,7 @@
             vmem((2, tiles) + tile, F32),
             vmem((8, 9) + double, F32),
             vmem((2,) + tile, F32),
-            vmem((2, 16, width), F32),
+            vmem((2, FIELDS, 1, width), F32),
             vmem((FIELDS, 8) + tile, F32),
             vmem((2, width), F32),
             vmem((count, 2, width), F32),
@@ -569,18 +637,15 @@
             vmem((8, width), F32),
             vmem((4, tiles) + tile, F32),
             vmem((2,) + tile, F32),
-            vmem((2, 16, width), F32),
+            vmem((2, FIELDS, 1, width), F32),
             vmem((4, 1, width), F32),
+            vmem((3,) + tile, F32),
+            vmem((3,) + tile, F32),
+            vmem((max(planes * height, 1024 + 3 * count), 1, width), F32),
+            dma((3,)),
+            dma(()),
             dma((7,)),
-            dma((8, 2)),
-            dma((8, 2)),
-            dma((8,)),
-            dma((8,)),
-            dma(()),
-            dma(()),
-            dma(()),
-            dma(()),
-            pltpu.SemaphoreType.REGULAR,
+            pltpu.SemaphoreType.REGULAR((len(rounds_of(plane_width(wide), narrow)),)),
         ],
         compiler_params=pltpu.CompilerParams(collective_id=0, has_side_effects=True, vmem_limit_bytes=VMEM_LIMIT),
     )(*(
@@ -598,7 +663,7 @@
         scratch_shapes=[
             vmem(results[0].shape, F32),
             vmem(results[1].shape, F32),
-            dma((edge_count + 3,)),
+            dma((3,)),
         ],
         compiler_params=pltpu.CompilerParams(vmem_limit_bytes=VMEM_LIMIT),
     )(*staged)

time: 18.3 us -> 16.1 us (0.88)
  Pallas kernels: 17.5 us -> 15.3 us
    pallas_call x1, Pallas kernels: 16.6 us -> 14.5 us  [local(): pl.pallas_call(functools.partial(kernel, wide, narrow, share), out_shape=...]
where the time goes in v2:
time: 16.1 us; the launch traced here: 16 us
  Pallas kernels  15.3 us (95%)
  between operations  0.64 us (4%)
    pallas_call x1, Pallas kernels, local(): pl.pallas_call(functools.partial(kernel, wide, narrow, share), out_shape=...  14.5 us
    pallas_call x1, Pallas kernels, local(): pl.pallas_call(finish, out_shape=results, in_specs=[pl.BlockSpec(memory_s...  0.82 us

profile of v2, /device:TPU:0, one launch (start us, length us, event | category | flops | bytes accessed | tf_op | source)
XLA Modules:
  0.0 16.0 jit_solution(880687240814791296)
XLA Ops:
  0.6 14.5 %shard_map.94 = (f32[7,6,3,8,128]{4,3,2,1,0:T(8,128)S(1)}, f32[9,8,128]{2,1,0:T(8,128)S(1)}, f32[3,8,128]{2,1,0:T(8,128)S(1)}, f32[2,8,128]{2,1,0:T(8,128)S(1)}, f32[16,36]{1,0:T(8,128)S(1)}) custom-call(f32[3,8,128]{2,1,0:T(8,128)} %coords_h.1, s32[8,128]{1,0:T(8,128)} %member_h.1, f32[3,8,128]{2,1,0:T(8,128)} %start_h.1, f32[9,8,128]{2,1,0:T(8,128)} %bitcast.4, ...), custom_call_target="tpu_custom_call" | custom-call | tf_op jit(solution)/shard_map/pallas_call | solution.py:611
  15.2 0.8 %shard_map.95 = (f32[7,6,3,8,128]{4,3,2,1,0:T(8,128)}, f32[3,8,128]{2,1,0:T(8,128)}, f32[16,36]{1,0:T(8,128)}) custom-call(f32[7,6,3,8,128]{4,3,2,1,0:T(8,128)S(1)} %get-tuple-element.11.raw, f32[9,8,128]{2,1,0:T(8,128)S(1)} %get-tuple-element.12.fields, f32[3,8,128]{2,1,0:T(8,128)S(1)} %get-tuple-element.13.iterate, ...), custom_call_target="tpu_custom_call" | custom-call | tf_op jit(solution)/shard_map/pallas_call | solution.py:658

commit v3 on v2

--- a/solution.py
+++ b/solution.py
@@ -14,6 +14,7 @@
 SUMS = 10
 FIELDS = 9
 START, SELF, NB = 0, 3, 12
+STENCIL = 81
 STEPS = [(-1, -1), (-1, 0), (-1, 1), (0, -1), (0, 1), (1, -1), (1, 0), (1, 1)]
 VMEM_LIMIT = 16 * 1024 * 1024
 
@@ -29,24 +30,23 @@
     return wide if best == 1 else best
 
 
-def edge_slots(planes, width):
-    per = width // (ITERS - 1)
-    tiles = pl.cdiv(planes - SELF, per)
-    slots = [(tiles, ITERS * p, ITERS) for p in range(SELF)]
-    slots += [(p // per, p % per * (ITERS - 1), ITERS - 1) for p in range(planes - SELF)]
-    return slots, tiles
+def edge_slots(planes, columns, width):
+    per = width // (2 * columns)
+    return [(p // per, p % per * 2 * columns) for p in range(planes)], pl.cdiv(planes, per)
 
 
 def rounds_of(across_plane, narrow):
-    offsets, reach = [1], 1
-    while reach < max(across_plane, narrow) - 1:
-        offsets.append(reach + 1)
-        reach = 2 * reach + 1
-    return offsets
-
-
-IN_ROWS, IN_COORDS, IN_MAP = range(3)
-SIDES, CORNERS, STARTS, BANDS, EDGES, GATHER, TOTALS = range(7)
+    def doubled(size):
+        steps = [1]
+        while 2 * steps[-1] < size:
+            steps.append(2 * steps[-1])
+        return steps
+
+    return [(0, 1)] + [(step, 0) for step in doubled(across_plane)] + [(0, step) for step in doubled(narrow)[1:]]
+
+
+IN_NODES, IN_MAP = range(2)
+SIDES, CORNERS, BANDS, EDGES, GATHER, TOTALS = range(6)
 
 
 def kernel(
@@ -55,7 +55,7 @@
     out_ref, fields, iter_ref, scale_ref, coarse_ref,
     coords, member, nbr, cmap,
     ext, wpack, stencil, pack, tedges, disp, mine, gath, sumrow, allsum, partial,
-    wrecv, htrecv, vtrecv, ctrecv, firsts_own, firsts,
+    cpack, wrecv, erecv, crecv, srecv, htrecv, vtrecv, ctrecv, firsts_own, firsts,
     tally, in_sem, send_sem, recv_sem, round_sem,
 ):
     count = wide * narrow
@@ -70,8 +70,11 @@
     edge_count = nbr.shape[0]
     codes_at = NB + 9 * edge_count
     planes = codes_at + edge_count
-    slots, tiles = edge_slots(planes, width)
-    offsets = rounds_of(across_plane, narrow)
+    deep = ITERS - 1
+    start_slots, _ = edge_slots(SELF, ITERS, width)
+    slots, tiles = edge_slots(planes - SELF, deep, width)
+    stencil_slots, stencil_tiles = edge_slots(STENCIL, deep, width)
+    rounds = rounds_of(across_plane, narrow)
     right, left = 0, 1
 
     def exists(code):
@@ -105,8 +108,8 @@
     loads = [
         pltpu.make_async_copy(src, dst, in_sem.at[i])
         for src, dst, i in (
-            (nb_h, own(NB, nb_h.shape[0]), IN_ROWS), (self_h, own(SELF, 9), IN_ROWS), (start_h, own(START, 3), IN_ROWS),
-            (nbr_h, nbr, IN_ROWS), (coords_h, coords, IN_COORDS), (member_h, member, IN_COORDS), (cmap_h, cmap, IN_MAP),
+            (nb_h, own(NB, nb_h.shape[0]), IN_NODES), (self_h, own(SELF, 9), IN_NODES), (start_h, own(START, 3), IN_NODES),
+            (nbr_h, nbr, IN_NODES), (coords_h, coords, IN_NODES), (member_h, member, IN_NODES), (cmap_h, cmap, IN_MAP),
         )
     ]
     for load in loads:
@@ -126,38 +129,32 @@
                 if rows:
                     pl.when(jnp.logical_and(sides_here == a, ends_here == b))(functools.partial(wait_rows, sem, rows))
 
-    for code in (0, 2, 5, 7, 3, 4):
+    for code in (3, 4):
         expected = expected + greet(present_at[code], target(code))
 
     for p in range(plane_count):
         w = p * across_plane + me_q
         expected = expected + greet(jnp.abs(w - me_w) > 1, (w, me_n))
 
-    def partners(offset):
-        for dq in (-offset, 0, offset):
-            for dn in (-offset, 0, offset):
-                if (dq, dn) != (0, 0) and abs(dq) < across_plane and abs(dn) < narrow:
-                    q, n = me_q + dq, me_n + dn
-                    fits = [cond for step, cond in (
-                        (-dq, q >= 0), (dq, q < across_plane), (-dn, n >= 0), (dn, n < narrow),
-                    ) if step > 0]
-                    yield functools.reduce(jnp.logical_and, fits), (me_w + dq, n)
+    def partners(number):
+        for way in (-1, 1):
+            dq, dn = (way * step for step in rounds[number])
+            q, n = me_q + dq, me_n + dn
+            yield jnp.logical_and(jnp.logical_and(q >= 0, q < across_plane), jnp.logical_and(n >= 0, n < narrow)), (me_w + dq, n)
 
     def tell(number):
-        for cond, device in partners(offsets[number]):
+        for cond, device in partners(number):
             @pl.when(cond)
             def _(device=device):
                 pl.semaphore_signal(round_sem.at[number], inc=1, device_id=device, device_id_type=MESH)
 
     def hear(number):
-        pl.semaphore_wait(round_sem.at[number], sum(cond.astype(jnp.int32) for cond, _ in partners(offsets[number])))
-
-    deep = ITERS - 1
-
-    def corner_refs(ref, low):
+        pl.semaphore_wait(round_sem.at[number], sum(cond.astype(jnp.int32) for cond, _ in partners(number)))
+
+    def corner_refs(operator, start, low):
         at = 0 if low else height - deep
         start_at = 0 if low else height - ITERS
-        return [ref.at[0:tiles, at : at + deep, :], ref.at[tiles, start_at : start_at + ITERS, :]]
+        return [operator.at[:, at : at + deep, :], start.at[start_at : start_at + ITERS, :]]
 
     for code in range(8):
         dy, dx = STEPS[code]
@@ -170,14 +167,12 @@
                 vtrecv[0 if dy < 0 else 1] = jnp.zeros(vtrecv.shape[1:], F32)
                 at = deep - 1 if dy > 0 else height - deep
                 firsts[:, at : at + 1, :] = jnp.zeros((3, 1, width), F32)
-                at = deep if dy > 0 else height - deep - 1
-                for to in (right, left):
-                    wrecv[2 + to, 0:tiles, at : at + 1, :] = jnp.zeros((tiles, 1, width), F32)
+                erecv[:, at : at + 1, :] = jnp.zeros((tiles, 1, width), F32)
             elif dy == 0:
                 wrecv[side] = jnp.zeros(wrecv.shape[1:], F32)
                 htrecv[side] = jnp.zeros(htrecv.shape[1:], F32)
             else:
-                for ref in corner_refs(wrecv.at[2 + side], dy > 0):
+                for ref in corner_refs(crecv.at[side], srecv.at[side], dy > 0):
                     ref[...] = jnp.zeros(ref.shape, F32)
                 ctrecv[2 * side + (0 if dy < 0 else 1)] = jnp.zeros(ctrecv.shape[1:], F32)
 
@@ -185,12 +180,11 @@
     row = lax.broadcasted_iota(jnp.int32, shape, 0)
     first, last = lane == 0, lane == width - 1
 
-    wait_rows(in_sem.at[IN_ROWS], planes * height)
+    pl.semaphore_wait(barrier, expected)
+    tell(0)
+    wait_rows(in_sem.at[IN_NODES], (planes + 4) * height)
     for k in range(edge_count):
         ext[codes_at + k, 0:height, 0:width] = nbr[k].astype(F32)
-
-    pl.semaphore_wait(barrier, expected)
-    tell(0)
 
     def send(code, pairs, group):
         made = [
@@ -206,7 +200,10 @@
             for copy in made:
                 copy.start()
 
-    bands = ((START, 3, ITERS), (SELF, 9, deep - 1), (NB, planes - NB, deep - 1))
+    half = 9 * (edge_count // 2)
+    bands = (
+        (START, 3, ITERS), (SELF, 9, deep - 1), (NB, half, deep - 1), (NB + half, planes - NB - half, deep - 1),
+    )
 
     def band_pairs(code, band):
         base, size, rows = band
@@ -217,40 +214,39 @@
         )]
 
     def end_pairs(code):
-        here, there = (deep - 1, deep) if STEPS[code][0] < 0 else (height - deep, height - deep - 1)
-        return [
-            (wpack.at[side, 0:tiles, here : here + 1, :], wrecv.at[3 - side, 0:tiles, there : there + 1, :])
-            for side in (right, left)
-        ]
+        here = deep - 1 if STEPS[code][0] < 0 else height - deep
+        return [(wpack.at[0:tiles, here : here + 1, :], erecv.at[:, here : here + 1, :])]
 
     def first_pairs(code):
         here = deep - 1 if STEPS[code][0] < 0 else height - deep
         return [(firsts_own.at[:, here : here + 1, :], firsts.at[:, here : here + 1, :])]
 
     for code in (1, 6):
-        send(code, band_pairs(code, bands[0]), STARTS)
+        send(code, band_pairs(code, bands[0]), SIDES)
         send(code, band_pairs(code, bands[1]), BANDS)
-    for side in (right, left):
-        packed = [jnp.zeros(shape, F32) for _ in range(tiles + 1)]
-        for p, (t, at, columns) in enumerate(slots):
-            begin = 0 if side == left else width - columns
-            moved = roll(ext[p, 0:height, 0:width], at - begin, 1)
-            packed[t] = moved if at == 0 else jnp.where(lane >= at, moved, packed[t])
-        for t in range(tiles + 1):
-            wpack[side, t] = packed[t]
-
-    for code in (0, 2, 5, 7, 3, 4):
-        dy, dx = STEPS[code]
-        mine_side, their_side = (left, right) if dx < 0 else (right, left)
-        if dy == 0:
-            send(code, [(wpack.at[mine_side], wrecv.at[their_side])], SIDES)
-        else:
-            send(code, list(zip(
-                corner_refs(wpack.at[mine_side], dy < 0), corner_refs(wrecv.at[2 + their_side], dy < 0),
-            )), CORNERS)
+    def packed(sources, slots, columns):
+        result = []
+        for source, (t, at) in zip(sources, slots):
+            moved = roll(source(), at + columns, 1)
+            if at == 0:
+                result.append(moved)
+            else:
+                result[t] = jnp.where(lane >= at, moved, result[t])
+        return result
+
+    def main(p):
+        return lambda: ext[p, 0:height, 0:width]
+
+    raw = packed([main(SELF + p) for p in range(planes - SELF)], slots, deep)
+    starts = packed([main(START + r) for r in range(SELF)], start_slots, ITERS)
+    for t, value in enumerate(raw + starts):
+        wpack[t] = value
+
     for code in (1, 6):
-        send(code, end_pairs(code), CORNERS)
-        send(code, band_pairs(code, bands[2]), BANDS)
+        send(code, end_pairs(code), SIDES)
+        send(code, band_pairs(code, bands[2]) + band_pairs(code, bands[3]), BANDS)
+    for code in (3, 4):
+        send(code, [(wpack, wrecv.at[left if code == 4 else right])], SIDES)
 
     def by_displacement(r0, c0):
         def at(p):
@@ -281,14 +277,26 @@
         return applied
 
     by_displacement(0, 0)
+    shifted_main = [main(SELF + q) for q in range(9)] + [
+        lambda code=code, q=q: stencil[code, q, 0:height, 0:width] for code in range(8) for q in range(9)
+    ]
+    for t, value in enumerate(packed(shifted_main, stencil_slots, deep)):
+        cpack[t] = value
     inside_rows, inside_cols = slice(0, height), slice(0, width)
     applied = apply([ext[START + r, 0:height, 0:width] for r in range(3)], inside_rows, inside_cols)
     for r in range(3):
         firsts_own[r] = applied[r] * (1.0 / ext[SELF + 4 * r, 0:height, 0:width])
+    hear(0)
+    tell(1)
+    for code in (0, 2, 5, 7):
+        dy, dx = STEPS[code]
+        side = right if dx < 0 else left
+        send(code, list(zip(
+            corner_refs(cpack, wpack.at[tiles], dy < 0), corner_refs(crecv.at[side], srecv.at[side], dy < 0),
+        )), CORNERS)
     for code in (1, 6):
         send(code, first_pairs(code), BANDS)
 
-    wait_rows(in_sem.at[IN_COORDS], 4 * height)
     present = member[...].astype(F32)
     x, y, z = (coords[r] * present for r in range(3))
     products = [present * present, x * present, y * present, z * present, x * x, y * y, z * z, x * y, x * z, y * z]
@@ -357,28 +365,37 @@
             dst = ctrecv.at[2 * their_side + (1 if dy < 0 else 0)]
         send(code, [(src, dst)], EDGES)
 
-    for number in range(len(offsets) - 1):
+    for number in range(1, len(rounds) - 1):
         hear(number)
         tell(number + 1)
-    def unpack(part, r0):
-        for p, (t, at, columns) in enumerate(slots):
-            from_right = roll(wrecv[part + right, t], -at, 1)
-            from_left = roll(wrecv[part + left, t], -at - columns, 1)
-            both = jnp.where(lane < width // 2, from_right, from_left)
-            ext[p, r0 : r0 + height, width:] = both
-            if part and p >= SELF:
-                ext[p, height + deep - 1 : height + deep, 0:width] = both[deep : deep + 1]
-                ext[p, 2 * height - deep : 2 * height - deep + 1, 0:width] = both[height - deep - 1 : height - deep]
+    def joined(from_left, from_right, columns):
+        takes_left = lax.rem(lane, 2 * columns) < columns
+        return [jnp.where(takes_left, a[...], b[...]) for a, b in zip(from_left, from_right)]
+
+    def tiles_of(ref, count_of):
+        return [ref.at[t] for t in range(count_of)]
+
+    def unpack_starts(r0, from_left, from_right):
+        both, = joined([from_left], [from_right], ITERS)
+        for r, (_, at) in enumerate(start_slots):
+            ext[START + r, r0 : r0 + height, width:] = roll(both, -at - ITERS, 1)
 
     side_rows, start_rows = (tiles + 1) * height, SELF * ITERS
-    corner_rows, end_rows = tiles * deep + ITERS, 2 * tiles
+    corner_rows, end_rows = stencil_tiles * deep + ITERS, tiles
     band_rows = (planes - SELF) * (deep - 1) + 3
     edge_rows = (height, FIELDS, 1)
-    wait_halo(recv_sem.at[SIDES], side_rows, 0, 0)
-    unpack(0, 0)
+    wait_halo(recv_sem.at[SIDES], side_rows, end_rows + start_rows, 0)
+    unpack_starts(0, wrecv.at[left, tiles], wrecv.at[right, tiles])
+    both = joined(tiles_of(wrecv.at[left], tiles), tiles_of(wrecv.at[right], tiles), deep)
+    for p, (t, at) in enumerate(slots):
+        ext[SELF + p, 0:height, width:] = roll(both[t], -at - deep, 1)
+        ends = roll(erecv[t], -at - deep, 1)
+        ext[SELF + p, height + deep - 1 : height + deep, 0:width] = ends[deep - 1 : deep]
+        ext[SELF + p, 2 * height - deep : 2 * height - deep + 1, 0:width] = ends[height - deep : height - deep + 1]
     by_displacement(0, width)
 
-    hear(len(offsets) - 1)
+    if len(rounds) > 1:
+        hear(len(rounds) - 1)
 
     def to_all(src, dst, group):
         def one(i):
@@ -401,10 +418,15 @@
 
     to_all(mine, gath.at[me], GATHER)
 
-    wait_halo(recv_sem.at[CORNERS], 0, end_rows, corner_rows)
-    unpack(2, height)
-    by_displacement(height, width)
-    wait_halo(recv_sem.at[STARTS], 0, start_rows, 0)
+    wait_halo(recv_sem.at[CORNERS], 0, 0, corner_rows)
+    unpack_starts(height, srecv.at[left], srecv.at[right])
+    both = joined(tiles_of(crecv.at[left], stencil_tiles), tiles_of(crecv.at[right], stencil_tiles), deep)
+    for p, (t, at) in enumerate(stencil_slots):
+        value = roll(both[t], -at - deep, 1)
+        if p < 9:
+            ext[SELF + p, height:, width:] = value
+        else:
+            stencil[(p - 9) // 9, (p - 9) % 9, height:, width:] = value
     whole_cols, beyond = slice(None), slice(width, None)
     begin = [ext[START + r] for r in range(3)]
     begin_top = apply(begin, inside_rows, whole_cols)
@@ -600,7 +622,8 @@
     tile = (height, width)
     double = (2 * height, 2 * width)
     planes = 12 + 10 * edge_count
-    tiles = edge_slots(planes, width)[1] + 1
+    tiles = edge_slots(planes - SELF, ITERS - 1, width)[1]
+    stencil_tiles = edge_slots(STENCIL, ITERS - 1, width)[1]
     vmem = pltpu.VMEM
     dma = pltpu.SemaphoreType.DMA
     results = (
@@ -625,7 +648,7 @@
             vmem((edge_count,) + tile, jnp.int32),
             pltpu.SMEM(coarse_map.shape, jnp.int32),
             vmem((planes,) + double, F32),
-            vmem((2, tiles) + tile, F32),
+            vmem((tiles + 1,) + tile, F32),
             vmem((8, 9) + double, F32),
             vmem((2,) + tile, F32),
             vmem((2, FIELDS, 1, width), F32),
@@ -635,16 +658,20 @@
             vmem((1, width), F32),
             vmem((count, 1, width), F32),
             vmem((8, width), F32),
-            vmem((4, tiles) + tile, F32),
+            vmem((stencil_tiles,) + tile, F32),
+            vmem((2, tiles + 1) + tile, F32),
+            vmem((tiles,) + tile, F32),
+            vmem((2, stencil_tiles) + tile, F32),
+            vmem((2,) + tile, F32),
             vmem((2,) + tile, F32),
             vmem((2, FIELDS, 1, width), F32),
             vmem((4, 1, width), F32),
             vmem((3,) + tile, F32),
             vmem((3,) + tile, F32),
-            vmem((max(planes * height, 1024 + 3 * count), 1, width), F32),
-            dma((3,)),
+            vmem((max((planes + 4) * height, 1024 + 3 * count), 1, width), F32),
+            dma((2,)),
             dma(()),
-            dma((7,)),
+            dma((6,)),
             pltpu.SemaphoreType.REGULAR((len(rounds_of(plane_width(wide), narrow)),)),
         ],
         compiler_params=pltpu.CompilerParams(collective_id=0, has_side_effects=True, vmem_limit_bytes=VMEM_LIMIT),

time: 16.1 us -> 15.6 us (0.969)
  Pallas kernels: 15.3 us -> 14.8 us
    pallas_call x1, Pallas kernels: 14.5 us -> 14 us  [local(): pl.pallas_call(functools.partial(kernel, wide, narrow, share), out_shape=...]
where the time goes in v3:
time: 15.6 us; the launch traced here: 15.5 us
  Pallas kernels  14.8 us (95%)
  between operations  0.64 us (4%)
    pallas_call x1, Pallas kernels, local(): pl.pallas_call(functools.partial(kernel, wide, narrow, share), out_shape=...  14 us
    pallas_call x1, Pallas kernels, local(): pl.pallas_call(finish, out_shape=results, in_specs=[pl.BlockSpec(memory_s...  0.82 us

profile of v3, /device:TPU:0, one launch (start us, length us, event | category | flops | bytes accessed | tf_op | source)
XLA Modules:
  0.0 15.5 jit_solution(13495315696935599304)
XLA Ops:
  0.6 14.0 %shard_map.94 = (f32[7,6,3,8,128]{4,3,2,1,0:T(8,128)S(1)}, f32[9,8,128]{2,1,0:T(8,128)S(1)}, f32[3,8,128]{2,1,0:T(8,128)S(1)}, f32[2,8,128]{2,1,0:T(8,128)S(1)}, f32[16,36]{1,0:T(8,128)S(1)}) custom-call(f32[3,8,128]{2,1,0:T(8,128)} %coords_h.1, s32[8,128]{1,0:T(8,128)} %member_h.1, f32[3,8,128]{2,1,0:T(8,128)} %start_h.1, f32[9,8,128]{2,1,0:T(8,128)} %bitcast.4, ...), custom_call_target="tpu_custom_call" | custom-call | tf_op jit(solution)/shard_map/pallas_call | solution.py:634
  14.6 0.8 %shard_map.95 = (f32[7,6,3,8,128]{4,3,2,1,0:T(8,128)}, f32[3,8,128]{2,1,0:T(8,128)}, f32[16,36]{1,0:T(8,128)}) custom-call(f32[7,6,3,8,128]{4,3,2,1,0:T(8,128)S(1)} %get-tuple-element.11.raw, f32[9,8,128]{2,1,0:T(8,128)S(1)} %get-tuple-element.12.fields, f32[3,8,128]{2,1,0:T(8,128)S(1)} %get-tuple-element.13.iterate, ...), custom_call_target="tpu_custom_call" | custom-call | tf_op jit(solution)/shard_map/pallas_call | solution.py:685

commit v4 on v3

--- a/solution.py
+++ b/solution.py
@@ -46,7 +46,7 @@
 
 
 IN_NODES, IN_MAP = range(2)
-SIDES, CORNERS, BANDS, EDGES, GATHER, TOTALS = range(6)
+SIDES, ENDS, CORNERS, BANDS, EDGES, GATHER, TOTALS = range(7)
 
 
 def kernel(
@@ -55,7 +55,7 @@
     out_ref, fields, iter_ref, scale_ref, coarse_ref,
     coords, member, nbr, cmap,
     ext, wpack, stencil, pack, tedges, disp, mine, gath, sumrow, allsum, partial,
-    cpack, wrecv, erecv, crecv, srecv, htrecv, vtrecv, ctrecv, firsts_own, firsts,
+    cpack, wrecv, erecv, crecv, srecv, near, nrecv, htrecv, vtrecv, ctrecv, firsts_own, firsts,
     tally, in_sem, send_sem, recv_sem, round_sem,
 ):
     count = wide * narrow
@@ -156,6 +156,9 @@
         start_at = 0 if low else height - ITERS
         return [operator.at[:, at : at + deep, :], start.at[start_at : start_at + ITERS, :]]
 
+    for side, at in ((0, 1), (1, height - 2)):
+        nrecv[side, :, 0:at, :] = jnp.zeros((near.shape[0], at, width), F32)
+        nrecv[side, :, at + 1 :, :] = jnp.zeros((near.shape[0], height - at - 1, width), F32)
     for code in range(8):
         dy, dx = STEPS[code]
         @pl.when(jnp.logical_not(present_at[code]))
@@ -165,9 +168,11 @@
                 at = height if dy > 0 else height + ITERS
                 ext[:, at : at + ITERS, 0:width] = jnp.zeros((planes, ITERS, width), F32)
                 vtrecv[0 if dy < 0 else 1] = jnp.zeros(vtrecv.shape[1:], F32)
-                at = deep - 1 if dy > 0 else height - deep
-                firsts[:, at : at + 1, :] = jnp.zeros((3, 1, width), F32)
-                erecv[:, at : at + 1, :] = jnp.zeros((tiles, 1, width), F32)
+                at = 1 if dy > 0 else height - deep
+                firsts[:, at : at + deep - 1, :] = jnp.zeros((3, deep - 1, width), F32)
+                erecv[:, at : at + deep - 1, :] = jnp.zeros((tiles, deep - 1, width), F32)
+                at = 1 if dy > 0 else height - 2
+                nrecv[0 if dy > 0 else 1, :, at : at + 1, :] = jnp.zeros((near.shape[0], 1, width), F32)
             elif dy == 0:
                 wrecv[side] = jnp.zeros(wrecv.shape[1:], F32)
                 htrecv[side] = jnp.zeros(htrecv.shape[1:], F32)
@@ -200,10 +205,7 @@
             for copy in made:
                 copy.start()
 
-    half = 9 * (edge_count // 2)
-    bands = (
-        (START, 3, ITERS), (SELF, 9, deep - 1), (NB, half, deep - 1), (NB + half, planes - NB - half, deep - 1),
-    )
+    bands = ((START, 3, ITERS), (SELF, 9, 1), (NB, planes - NB, 1))
 
     def band_pairs(code, band):
         base, size, rows = band
@@ -213,16 +215,24 @@
             ext.at[base : base + size, there : there + rows, 0:width],
         )]
 
+    def far_rows(code):
+        at = 1 if STEPS[code][0] < 0 else height - deep
+        return slice(at, at + deep - 1)
+
     def end_pairs(code):
-        here = deep - 1 if STEPS[code][0] < 0 else height - deep
-        return [(wpack.at[0:tiles, here : here + 1, :], erecv.at[:, here : here + 1, :])]
+        at = far_rows(code)
+        return [(wpack.at[0:tiles, at, :], erecv.at[:, at, :])]
 
     def first_pairs(code):
-        here = deep - 1 if STEPS[code][0] < 0 else height - deep
-        return [(firsts_own.at[:, here : here + 1, :], firsts.at[:, here : here + 1, :])]
+        at = far_rows(code)
+        return [(firsts_own.at[:, at, :], firsts.at[:, at, :])]
+
+    def near_pairs(code):
+        at = 1 if STEPS[code][0] < 0 else height - 2
+        return [(near.at[:, at : at + 1, :], nrecv.at[0 if code == 1 else 1, :, at : at + 1, :])]
 
     for code in (1, 6):
-        send(code, band_pairs(code, bands[0]), SIDES)
+        send(code, band_pairs(code, bands[0]), ENDS)
         send(code, band_pairs(code, bands[1]), BANDS)
     def packed(sources, slots, columns):
         result = []
@@ -243,12 +253,12 @@
         wpack[t] = value
 
     for code in (1, 6):
-        send(code, end_pairs(code), SIDES)
-        send(code, band_pairs(code, bands[2]) + band_pairs(code, bands[3]), BANDS)
+        send(code, end_pairs(code), ENDS)
+        send(code, band_pairs(code, bands[2]), BANDS)
     for code in (3, 4):
         send(code, [(wpack, wrecv.at[left if code == 4 else right])], SIDES)
 
-    def by_displacement(r0, c0):
+    def by_displacement(r0, c0, sent=None):
         def at(p):
             return ext[p, r0 : r0 + height, c0 : c0 + width]
 
@@ -258,12 +268,16 @@
                 blocks = [at(NB + 9 * k + q) for k in range(edge_count)]
                 for code in (group, group + 1):
                     value = jnp.zeros(shape, F32)
+                    if sent is not None and code in (0, 1, 2):
+                        value = sent[0, 9 * code + q]
+                    elif sent is not None and code in (5, 6, 7):
+                        value = sent[1, 9 * (code - 5) + q]
                     for k in range(edge_count):
                         value = jnp.where(masks[code, k], blocks[k], value)
                     stencil[code, q, r0 : r0 + height, c0 : c0 + width] = value
 
-    def apply(iterate, rs, cs):
-        applied = [sum(ext[SELF + 3 * r + s, rs, cs] * iterate[s][rs, cs] for s in range(3)) for r in range(3)]
+    def apply_parts(iterate, rs, cs, split):
+        parts = {0: [sum(ext[SELF + 3 * r + s, rs, cs] * iterate[s][rs, cs] for s in range(3)) for r in range(3)]}
         for s in range(3):
             for dx in (0, -1, 1):
                 shifted = roll(iterate[s], -dx, 1)
@@ -272,20 +286,41 @@
                         continue
                     code = STEPS.index((dy, dx))
                     moved = roll(shifted, -dy, 0)[rs, cs]
+                    part = parts.setdefault(dy if split else 0, [None] * 3)
                     for r in range(3):
-                        applied[r] = applied[r] + stencil[code, 3 * r + s, rs, cs] * moved
-        return applied
+                        term = stencil[code, 3 * r + s, rs, cs] * moved
+                        part[r] = term if part[r] is None else part[r] + term
+        return parts
+
+    def apply(iterate, rs, cs):
+        return apply_parts(iterate, rs, cs, False)[0]
 
     by_displacement(0, 0)
+    inside_rows, inside_cols = slice(0, height), slice(0, width)
+    own_inverse = [1.0 / ext[SELF + 4 * r, 0:height, 0:width] for r in range(3)]
+    applied = apply([ext[START + r, 0:height, 0:width] for r in range(3)], inside_rows, inside_cols)
+    first_own = [applied[r] * own_inverse[r] for r in range(3)]
+    for r in range(3):
+        firsts_own[r] = first_own[r]
+    known = jnp.logical_and(lane > 1, lane < width - 2)
+    upper = row < height // 2
+    scale = [jnp.where(known, own_inverse[r], 0.0) for r in range(3)]
+    for c in range(3):
+        for q in range(9):
+            toward = jnp.where(upper, stencil[c, q, 0:height, 0:width], stencil[c + 5, q, 0:height, 0:width])
+            near[9 * c + q] = jnp.where(known, toward * scale[q // 3], 0.0)
+    split = apply_parts(first_own, inside_rows, inside_cols, True)
+    for r in range(3):
+        second = split[0][r] + jnp.where(upper, split[1][r], split[-1][r])
+        near[27 + r] = jnp.where(known, second * own_inverse[r], 0.0)
+    for code in (1, 6):
+        send(code, first_pairs(code) + near_pairs(code), BANDS)
+
     shifted_main = [main(SELF + q) for q in range(9)] + [
         lambda code=code, q=q: stencil[code, q, 0:height, 0:width] for code in range(8) for q in range(9)
     ]
     for t, value in enumerate(packed(shifted_main, stencil_slots, deep)):
         cpack[t] = value
-    inside_rows, inside_cols = slice(0, height), slice(0, width)
-    applied = apply([ext[START + r, 0:height, 0:width] for r in range(3)], inside_rows, inside_cols)
-    for r in range(3):
-        firsts_own[r] = applied[r] * (1.0 / ext[SELF + 4 * r, 0:height, 0:width])
     hear(0)
     tell(1)
     for code in (0, 2, 5, 7):
@@ -294,8 +329,6 @@
         send(code, list(zip(
             corner_refs(cpack, wpack.at[tiles], dy < 0), corner_refs(crecv.at[side], srecv.at[side], dy < 0),
         )), CORNERS)
-    for code in (1, 6):
-        send(code, first_pairs(code), BANDS)
 
     present = member[...].astype(F32)
     x, y, z = (coords[r] * present for r in range(3))
@@ -368,32 +401,6 @@
     for number in range(1, len(rounds) - 1):
         hear(number)
         tell(number + 1)
-    def joined(from_left, from_right, columns):
-        takes_left = lax.rem(lane, 2 * columns) < columns
-        return [jnp.where(takes_left, a[...], b[...]) for a, b in zip(from_left, from_right)]
-
-    def tiles_of(ref, count_of):
-        return [ref.at[t] for t in range(count_of)]
-
-    def unpack_starts(r0, from_left, from_right):
-        both, = joined([from_left], [from_right], ITERS)
-        for r, (_, at) in enumerate(start_slots):
-            ext[START + r, r0 : r0 + height, width:] = roll(both, -at - ITERS, 1)
-
-    side_rows, start_rows = (tiles + 1) * height, SELF * ITERS
-    corner_rows, end_rows = stencil_tiles * deep + ITERS, tiles
-    band_rows = (planes - SELF) * (deep - 1) + 3
-    edge_rows = (height, FIELDS, 1)
-    wait_halo(recv_sem.at[SIDES], side_rows, end_rows + start_rows, 0)
-    unpack_starts(0, wrecv.at[left, tiles], wrecv.at[right, tiles])
-    both = joined(tiles_of(wrecv.at[left], tiles), tiles_of(wrecv.at[right], tiles), deep)
-    for p, (t, at) in enumerate(slots):
-        ext[SELF + p, 0:height, width:] = roll(both[t], -at - deep, 1)
-        ends = roll(erecv[t], -at - deep, 1)
-        ext[SELF + p, height + deep - 1 : height + deep, 0:width] = ends[deep - 1 : deep]
-        ext[SELF + p, 2 * height - deep : 2 * height - deep + 1, 0:width] = ends[height - deep : height - deep + 1]
-    by_displacement(0, width)
-
     if len(rounds) > 1:
         hear(len(rounds) - 1)
 
@@ -418,6 +425,38 @@
 
     to_all(mine, gath.at[me], GATHER)
 
+    def joined(from_left, from_right, columns):
+        takes_left = lax.rem(lane, 2 * columns) < columns
+        return [jnp.where(takes_left, a[...], b[...]) for a, b in zip(from_left, from_right)]
+
+    def tiles_of(ref, count_of):
+        return [ref.at[t] for t in range(count_of)]
+
+    def unpack_starts(r0, from_left, from_right):
+        both, = joined([from_left], [from_right], ITERS)
+        for r, (_, at) in enumerate(start_slots):
+            ext[START + r, r0 : r0 + height, width:] = roll(both, -at - ITERS, 1)
+
+    side_rows, start_rows = (tiles + 1) * height, SELF * ITERS
+    corner_rows, end_rows = stencil_tiles * deep + ITERS, tiles * (deep - 1)
+    band_rows = planes - SELF + 3 * (deep - 1) + near.shape[0]
+    edge_rows = (height, FIELDS, 1)
+    wait_halo(recv_sem.at[SIDES], side_rows, 0, 0)
+    unpack_starts(0, wrecv.at[left, tiles], wrecv.at[right, tiles])
+    both = joined(tiles_of(wrecv.at[left], tiles), tiles_of(wrecv.at[right], tiles), deep)
+    for p, (t, at) in enumerate(slots):
+        ext[SELF + p, 0:height, width:] = roll(both[t], -at - deep, 1)
+    by_displacement(0, width)
+    wait_halo(recv_sem.at[ENDS], 0, end_rows + start_rows, 0)
+    for p, (t, at) in enumerate(slots):
+        ends = roll(erecv[t], -at - deep, 1)
+        if p < 9 or p >= codes_at - SELF:
+            ends = jnp.where(known, 0.0 if p < 9 else -1.0, ends)
+        for rows in (slice(1, deep), slice(height - deep, height - 1)):
+            ext[SELF + p, height + rows.start : height + rows.stop, 0:width] = ends[rows]
+
+    wait_halo(recv_sem.at[BANDS], 0, band_rows, 0)
+    by_displacement(height, 0, nrecv)
     wait_halo(recv_sem.at[CORNERS], 0, 0, corner_rows)
     unpack_starts(height, srecv.at[left], srecv.at[right])
     both = joined(tiles_of(crecv.at[left], stencil_tiles), tiles_of(crecv.at[right], stencil_tiles), deep)
@@ -431,8 +470,6 @@
     begin = [ext[START + r] for r in range(3)]
     begin_top = apply(begin, inside_rows, whole_cols)
     begin_corner = apply(begin, slice(height, None), beyond)
-    wait_halo(recv_sem.at[BANDS], 0, band_rows, 0)
-    by_displacement(height, 0)
 
     def full(p):
         return ext[p]
@@ -452,14 +489,18 @@
     inside = jnp.logical_and(
         jnp.logical_or(erow < last_row, erow >= back_row), jnp.logical_or(elane < last_lane, elane >= back_lane)
     )
-    inverse = [jnp.where(inside, 1.0 / full(SELF + 4 * r), 0.0) for r in range(3)]
+    far = jnp.logical_or(
+        jnp.logical_and(erow > height, erow < height + deep),
+        jnp.logical_and(erow > 2 * height - deep - 1, erow < 2 * height - 1),
+    )
+    far_known = jnp.logical_and(far, jnp.logical_and(elane > 1, elane < width - 2))
+    inverse = [
+        jnp.where(inside, 1.0 / jnp.where(far_known, 1.0, full(SELF + 4 * r)), 0.0) for r in range(3)
+    ]
     diag = [selfb[r, r]() for r in range(3)]
     inv = [inverse[r][:height, :width] for r in range(3)]
 
-    sent = jnp.logical_and(
-        jnp.logical_or(erow == height + deep - 1, erow == 2 * height - deep),
-        jnp.logical_and(elane > 0, elane < width - 1),
-    )
+    sent = jnp.logical_and(far, jnp.logical_and(elane > 0, elane < width - 1))
     spread = [
         jnp.concatenate([jnp.concatenate([firsts[r], firsts[r]], axis=0)] * 2, axis=1) for r in range(3)
     ]
@@ -483,6 +524,13 @@
         iterate = [applied[r] * (inv[r] if final else inverse[r]) for r in range(3)]
         if number == 0:
             iterate = [jnp.where(sent, spread[r], iterate[r]) for r in range(3)]
+        if number == 1:
+            rest = [nrecv[0, 27 + r] + nrecv[1, 27 + r] for r in range(3)]
+            iterate = [
+                jnp.concatenate([
+                    v[:height], jnp.concatenate([v[height:, :width] + rest[r], v[height:, width:]], axis=1),
+                ], axis=0) for r, v in enumerate(iterate)
+            ]
 
     totals = jnp.sum(partial[...], axis=1, keepdims=True)
     line = jnp.sum(jnp.where(lane == row, totals, 0.0), axis=0, keepdims=True)
@@ -663,6 +711,8 @@
             vmem((tiles,) + tile, F32),
             vmem((2, stencil_tiles) + tile, F32),
             vmem((2,) + tile, F32),
+            vmem((30,) + tile, F32),
+            vmem((2, 30) + tile, F32),
             vmem((2,) + tile, F32),
             vmem((2, FIELDS, 1, width), F32),
             vmem((4, 1, width), F32),
@@ -671,7 +721,7 @@
             vmem((max((planes + 4) * height, 1024 + 3 * count), 1, width), F32),
             dma((2,)),
             dma(()),
-            dma((6,)),
+            dma((7,)),
             pltpu.SemaphoreType.REGULAR((len(rounds_of(plane_width(wide), narrow)),)),
         ],
         compiler_params=pltpu.CompilerParams(collective_id=0, has_side_effects=True, vmem_limit_bytes=VMEM_LIMIT),

time: 15.6 us -> 15.6 us (level)
  no operation moved by 1% of the time
where the time goes in v4:
time: 15.6 us; the launch traced here: 15.4 us
  Pallas kernels  14.8 us (95%)
  between operations  0.64 us (4%)
    pallas_call x1, Pallas kernels, local(): pl.pallas_call(functools.partial(kernel, wide, narrow, share), out_shape=...  14 us
    pallas_call x1, Pallas kernels, local(): pl.pallas_call(finish, out_shape=results, in_specs=[pl.BlockSpec(memory_s...  0.82 us

profile of v4, /device:TPU:0, one launch (start us, length us, event | category | flops | bytes accessed | tf_op | source)
XLA Modules:
  0.0 15.4 jit_solution(106461986937906652)
XLA Ops:
  0.6 14.0 %shard_map.94 = (f32[7,6,3,8,128]{4,3,2,1,0:T(8,128)S(1)}, f32[9,8,128]{2,1,0:T(8,128)S(1)}, f32[3,8,128]{2,1,0:T(8,128)S(1)}, f32[2,8,128]{2,1,0:T(8,128)S(1)}, f32[16,36]{1,0:T(8,128)S(1)}) custom-call(f32[3,8,128]{2,1,0:T(8,128)} %coords_h.1, s32[8,128]{1,0:T(8,128)} %member_h.1, f32[3,8,128]{2,1,0:T(8,128)} %start_h.1, f32[9,8,128]{2,1,0:T(8,128)} %bitcast.4, ...), custom_call_target="tpu_custom_call" | custom-call | tf_op jit(solution)/shard_map/pallas_call | solution.py:682
  14.6 0.8 %shard_map.95 = (f32[7,6,3,8,128]{4,3,2,1,0:T(8,128)}, f32[3,8,128]{2,1,0:T(8,128)}, f32[16,36]{1,0:T(8,128)}) custom-call(f32[7,6,3,8,128]{4,3,2,1,0:T(8,128)S(1)} %get-tuple-element.11.raw, f32[9,8,128]{2,1,0:T(8,128)S(1)} %get-tuple-element.12.fields, f32[3,8,128]{2,1,0:T(8,128)S(1)} %get-tuple-element.13.iterate, ...), custom_call_target="tpu_custom_call" | custom-call | tf_op jit(solution)/shard_map/pallas_call | solution.py:735

commit v5 on v3

--- a/solution.py
+++ b/solution.py
@@ -46,7 +46,7 @@
 
 
 IN_NODES, IN_MAP = range(2)
-SIDES, CORNERS, BANDS, EDGES, GATHER, TOTALS = range(6)
+SIDES, ENDS, CORNERS, BANDS, EDGES, GATHER, TOTALS = range(7)
 
 
 def kernel(
@@ -200,10 +200,7 @@
             for copy in made:
                 copy.start()
 
-    half = 9 * (edge_count // 2)
-    bands = (
-        (START, 3, ITERS), (SELF, 9, deep - 1), (NB, half, deep - 1), (NB + half, planes - NB - half, deep - 1),
-    )
+    bands = ((START, 3, ITERS), (SELF, 9, deep - 1), (NB, 9 * (edge_count - 1), deep - 1), (codes_at - 9, 9 + edge_count, deep - 1))
 
     def band_pairs(code, band):
         base, size, rows = band
@@ -222,7 +219,7 @@
         return [(firsts_own.at[:, here : here + 1, :], firsts.at[:, here : here + 1, :])]
 
     for code in (1, 6):
-        send(code, band_pairs(code, bands[0]), SIDES)
+        send(code, band_pairs(code, bands[0]), ENDS)
         send(code, band_pairs(code, bands[1]), BANDS)
     def packed(sources, slots, columns):
         result = []
@@ -243,7 +240,7 @@
         wpack[t] = value
 
     for code in (1, 6):
-        send(code, end_pairs(code), SIDES)
+        send(code, end_pairs(code), ENDS)
         send(code, band_pairs(code, bands[2]) + band_pairs(code, bands[3]), BANDS)
     for code in (3, 4):
         send(code, [(wpack, wrecv.at[left if code == 4 else right])], SIDES)
@@ -286,6 +283,8 @@
     applied = apply([ext[START + r, 0:height, 0:width] for r in range(3)], inside_rows, inside_cols)
     for r in range(3):
         firsts_own[r] = applied[r] * (1.0 / ext[SELF + 4 * r, 0:height, 0:width])
+    for code in (1, 6):
+        send(code, first_pairs(code), BANDS)
     hear(0)
     tell(1)
     for code in (0, 2, 5, 7):
@@ -294,8 +293,6 @@
         send(code, list(zip(
             corner_refs(cpack, wpack.at[tiles], dy < 0), corner_refs(crecv.at[side], srecv.at[side], dy < 0),
         )), CORNERS)
-    for code in (1, 6):
-        send(code, first_pairs(code), BANDS)
 
     present = member[...].astype(F32)
     x, y, z = (coords[r] * present for r in range(3))
@@ -368,32 +365,6 @@
     for number in range(1, len(rounds) - 1):
         hear(number)
         tell(number + 1)
-    def joined(from_left, from_right, columns):
-        takes_left = lax.rem(lane, 2 * columns) < columns
-        return [jnp.where(takes_left, a[...], b[...]) for a, b in zip(from_left, from_right)]
-
-    def tiles_of(ref, count_of):
-        return [ref.at[t] for t in range(count_of)]
-
-    def unpack_starts(r0, from_left, from_right):
-        both, = joined([from_left], [from_right], ITERS)
-        for r, (_, at) in enumerate(start_slots):
-            ext[START + r, r0 : r0 + height, width:] = roll(both, -at - ITERS, 1)
-
-    side_rows, start_rows = (tiles + 1) * height, SELF * ITERS
-    corner_rows, end_rows = stencil_tiles * deep + ITERS, tiles
-    band_rows = (planes - SELF) * (deep - 1) + 3
-    edge_rows = (height, FIELDS, 1)
-    wait_halo(recv_sem.at[SIDES], side_rows, end_rows + start_rows, 0)
-    unpack_starts(0, wrecv.at[left, tiles], wrecv.at[right, tiles])
-    both = joined(tiles_of(wrecv.at[left], tiles), tiles_of(wrecv.at[right], tiles), deep)
-    for p, (t, at) in enumerate(slots):
-        ext[SELF + p, 0:height, width:] = roll(both[t], -at - deep, 1)
-        ends = roll(erecv[t], -at - deep, 1)
-        ext[SELF + p, height + deep - 1 : height + deep, 0:width] = ends[deep - 1 : deep]
-        ext[SELF + p, 2 * height - deep : 2 * height - deep + 1, 0:width] = ends[height - deep : height - deep + 1]
-    by_displacement(0, width)
-
     if len(rounds) > 1:
         hear(len(rounds) - 1)
 
@@ -417,6 +388,34 @@
             pl.loop(0, count)(one)
 
     to_all(mine, gath.at[me], GATHER)
+
+    def joined(from_left, from_right, columns):
+        takes_left = lax.rem(lane, 2 * columns) < columns
+        return [jnp.where(takes_left, a[...], b[...]) for a, b in zip(from_left, from_right)]
+
+    def tiles_of(ref, count_of):
+        return [ref.at[t] for t in range(count_of)]
+
+    def unpack_starts(r0, from_left, from_right):
+        both, = joined([from_left], [from_right], ITERS)
+        for r, (_, at) in enumerate(start_slots):
+            ext[START + r, r0 : r0 + height, width:] = roll(both, -at - ITERS, 1)
+
+    side_rows, start_rows = (tiles + 1) * height, SELF * ITERS
+    corner_rows, end_rows = stencil_tiles * deep + ITERS, tiles
+    band_rows = (planes - SELF) * (deep - 1) + 3
+    edge_rows = (height, FIELDS, 1)
+    wait_halo(recv_sem.at[SIDES], side_rows, 0, 0)
+    unpack_starts(0, wrecv.at[left, tiles], wrecv.at[right, tiles])
+    both = joined(tiles_of(wrecv.at[left], tiles), tiles_of(wrecv.at[right], tiles), deep)
+    for p, (t, at) in enumerate(slots):
+        ext[SELF + p, 0:height, width:] = roll(both[t], -at - deep, 1)
+    by_displacement(0, width)
+    wait_halo(recv_sem.at[ENDS], 0, end_rows + start_rows, 0)
+    for p, (t, at) in enumerate(slots):
+        ends = roll(erecv[t], -at - deep, 1)
+        ext[SELF + p, height + deep - 1 : height + deep, 0:width] = ends[deep - 1 : deep]
+        ext[SELF + p, 2 * height - deep : 2 * height - deep + 1, 0:width] = ends[height - deep : height - deep + 1]
 
     wait_halo(recv_sem.at[CORNERS], 0, 0, corner_rows)
     unpack_starts(height, srecv.at[left], srecv.at[right])
@@ -671,7 +670,7 @@
             vmem((max((planes + 4) * height, 1024 + 3 * count), 1, width), F32),
             dma((2,)),
             dma(()),
-            dma((6,)),
+            dma((7,)),
             pltpu.SemaphoreType.REGULAR((len(rounds_of(plane_width(wide), narrow)),)),
         ],
         compiler_params=pltpu.CompilerParams(collective_id=0, has_side_effects=True, vmem_limit_bytes=VMEM_LIMIT),

time: 15.6 us -> 15.6 us (level)
  no operation moved by 1% of the time
where the time goes in v5:
time: 15.6 us; the launch traced here: 15.5 us
  Pallas kernels  14.8 us (95%)
  between operations  0.64 us (4%)
    pallas_call x1, Pallas kernels, local(): pl.pallas_call(functools.partial(kernel, wide, narrow, share), out_shape=...  14 us
    pallas_call x1, Pallas kernels, local(): pl.pallas_call(finish, out_shape=results, in_specs=[pl.BlockSpec(memory_s...  0.82 us

profile of v5, /device:TPU:0, one launch (start us, length us, event | category | flops | bytes accessed | tf_op | source)
XLA Modules:
  0.0 15.5 jit_solution(8266012878301028818)
XLA Ops:
  0.6 14.0 %shard_map.94 = (f32[7,6,3,8,128]{4,3,2,1,0:T(8,128)S(1)}, f32[9,8,128]{2,1,0:T(8,128)S(1)}, f32[3,8,128]{2,1,0:T(8,128)S(1)}, f32[2,8,128]{2,1,0:T(8,128)S(1)}, f32[16,36]{1,0:T(8,128)S(1)}) custom-call(f32[3,8,128]{2,1,0:T(8,128)} %coords_h.1, s32[8,128]{1,0:T(8,128)} %member_h.1, f32[3,8,128]{2,1,0:T(8,128)} %start_h.1, f32[9,8,128]{2,1,0:T(8,128)} %bitcast.4, ...), custom_call_target="tpu_custom_call" | custom-call | tf_op jit(solution)/shard_map/pallas_call | solution.py:633
  14.6 0.8 %shard_map.95 = (f32[7,6,3,8,128]{4,3,2,1,0:T(8,128)}, f32[3,8,128]{2,1,0:T(8,128)}, f32[16,36]{1,0:T(8,128)}) custom-call(f32[7,6,3,8,128]{4,3,2,1,0:T(8,128)S(1)} %get-tuple-element.11.raw, f32[9,8,128]{2,1,0:T(8,128)S(1)} %get-tuple-element.12.fields, f32[3,8,128]{2,1,0:T(8,128)S(1)} %get-tuple-element.13.iterate, ...), custom_call_target="tpu_custom_call" | custom-call | tf_op jit(solution)/shard_map/pallas_call | solution.py:684
